TPU v7x, 256 devices: a whole 4x4x8 slice. The times are simulated.
256 devices in a mesh: row: 64 (over z, y, core), col: 4 (over x).
Axes of the slice: x: 4, y: 4, z: 8, core: 2. Of those that a mesh axis runs over, the one named last changes fastest.
Arguments:
- pair_act: bfloat16 [768, 768, 128], P('row', 'col'), may hold values from -6 to 6
- tile_mask: int32 [12, 12], replicated, may hold values 0 or 1
- w_left_gate: bfloat16 [128, 128], replicated, may hold values from -0.5 to 0.5
- w_left: bfloat16 [128, 128], replicated, may hold values from -0.5 to 0.5
- w_right_gate: bfloat16 [128, 128], replicated, may hold values from -0.5 to 0.5
- w_right: bfloat16 [128, 128], replicated, may hold values from -0.5 to 0.5
- w_out_gate: bfloat16 [128, 128], replicated, may hold values from -0.5 to 0.5
- w_out: bfloat16 [128, 128], replicated, may hold values from -0.5 to 0.5
Outputs:
- update: bfloat16 [768, 768, 128], P('row', 'col')
All inputs are finite; a program needn't handle non-finite values.
Results may differ from a plain program's by a relative error of at most 0.0083.
Values may be sent and summed in bfloat16 or wider, within the bound.
A program may use at most 64 MiB of HBM per device.

v0:
```python
import jax
import jax.numpy as jnp
from jax import lax
from jax.sharding import PartitionSpec as P

TILES = 12


def in_one_piece(arrays, axis, split_dim, concat_dim, along):
    widths = [a.shape[along] for a in arrays]
    both = jnp.concatenate(arrays, axis=along)
    result = lax.all_to_all(both, axis, split_axis=split_dim, concat_axis=concat_dim, tiled=True)
    return tuple(jnp.split(result, [sum(widths[:k]) for k in range(1, len(widths))], axis=along))


def laid_out(parts, dim):
    lengths = list(parts.shape[1:])
    lengths[dim] *= parts.shape[0]
    return jnp.moveaxis(parts, 0, dim).reshape(lengths)


def copy_for_each(shard, axis):
    copies = jnp.broadcast_to(shard, (lax.axis_size(axis), *shard.shape))
    return lax.all_to_all(copies, axis, split_axis=0, concat_axis=0, tiled=True)


def collect(shard, axis, dim):
    return laid_out(copy_for_each(shard, axis), dim)


def norm_axis(values, axis):
    mean = jnp.mean(values, axis=axis, keepdims=True)
    centred = values - mean
    spread = jnp.mean(centred * centred, axis=axis, keepdims=True)
    return centred * lax.rsqrt(spread + 1e-05)


def local(pair_act, tile_mask, w_left_gate, w_left, w_right_gate, w_right, w_out_gate, w_out):
    rows, cols, width = pair_act.shape
    residues = rows * lax.axis_size("row")
    tile = residues // TILES
    normed = norm_axis(pair_act.astype(jnp.float32), 2).astype(jnp.bfloat16)
    tile_range = lax.iota(jnp.int32, TILES)
    row_ids = (lax.axis_index("row") * rows + lax.iota(jnp.int32, rows)) // tile
    col_ids = (lax.axis_index("col") * cols + lax.iota(jnp.int32, cols)) // tile
    row_hot = (row_ids[:, None] == tile_range[None, :]).astype(jnp.float32)
    col_hot = (col_ids[:, None] == tile_range[None, :]).astype(jnp.float32)
    pair_mask = jnp.dot(
        jnp.dot(row_hot, tile_mask.astype(jnp.float32), preferred_element_type=jnp.float32),
        col_hot.T,
        preferred_element_type=jnp.float32,
    )

    def project(weight):
        return jnp.einsum("ijd,de->eij", normed, weight, preferred_element_type=jnp.float32)

    left = (jax.nn.sigmoid(project(w_left_gate)) * project(w_left) * pair_mask[None]).astype(
        jnp.bfloat16
    )
    right = (jax.nn.sigmoid(project(w_right_gate)) * project(w_right) * pair_mask[None]).astype(
        jnp.bfloat16
    )
    left_rows, right_rows = in_one_piece((left, right), "row", 0, 1, 2)
    right_block = lax.all_to_all(right_rows, "col", split_axis=1, concat_axis=2, tiled=True)
    triangle = jnp.einsum(
        "cik,cjk->jci",
        collect(left_rows, "col", 2),
        right_block,
        preferred_element_type=jnp.float32,
    )
    triangle = triangle.astype(jnp.bfloat16)
    owned = lax.all_to_all(triangle, "row", split_axis=2, concat_axis=1, tiled=True)
    scaled = norm_axis(owned.astype(jnp.float32), 1).astype(jnp.bfloat16)
    projected = jnp.einsum("jci,ce->ije", scaled, w_out, preferred_element_type=jnp.float32)
    gate = jax.nn.sigmoid(
        jnp.einsum("ijd,de->ije", normed, w_out_gate, preferred_element_type=jnp.float32)
    )
    return (gate * projected).astype(jnp.bfloat16)


def solution(mesh):
    return jax.shard_map(
        local,
        mesh=mesh,
        in_specs=(P("row", "col", None), P(), P(), P(), P(), P(), P(), P()),
        out_specs=P("row", "col", None),
        check_vma=False,
    )
```

profile of v0, /device:TPU:1, one launch (start us, length us, event | category | flops | bytes accessed | tf_op | source)
XLA Modules:
  0.0 158.3 jit_solution(10255889193567638645)
XLA Ops:
  0.0 1.4 convert_reduce_fusion
  1.4 1.9 %fusion.20 = f32[12,192]{1,0:T(8,128)S(1)} fusion(bf16[12,192,128]{2,1,0:T(8,128)(2,1)} %param.8, f32[12,192]{1,0:T(8,128)S(1)} %broadcast_multiply_fusion.1), kind=kLoop, calls=%fused_computation.32 | loop fusion | flops 1177344 | bytes 608256 | tf_op jit(solution)/shard_map/reduce_sum | solution.py:34
  3.4 1.5 fusion.7
  5.0 1.5 fusion.10
  6.8 1.3 fusion.18
  8.0 1.3 fusion.19
  9.3 1.1 pad_maximum_fusion
  10.4 2.2 %copy.20 = bf16[128,12,384]{2,1,0:T(8,128)(2,1)S(1)} copy(bf16[128,12,384]{0,2,1:T(8,128)(2,1)} %pad_maximum_fusion) | data formatting | bytes 2359296 | tf_op jit(solution)/shard_map/concatenate | solution.py:11
  12.6 52.0 %all_to_all.50 = bf16[128,12,384]{2,1,0:T(8,128)(2,1)S(1)} all-to-all(bf16[128,12,384]{2,1,0:T(8,128)(2,1)S(1)} %copy.20), channel_id=1, replica_groups=mesh['row'=64,'col'=4] {'row'}, dimensions={0} | all-to-all | bytes 2359296 | tf_op jit(solution)/shard_map/all_to_all | solution.py:12
  65.5 2.4 %fusion.44 = (bf16[2,768,192]{2,0,1:T(2,128)(2,1)S(1)}, bf16[2,768,192]{2,0,1:T(2,128)(2,1)}) fusion(bf16[2,768,384]{2,0,1:T(2,128)(2,1)S(1)} %bitcast.59), kind=kLoop, calls=%fused_computation.64 | loop fusion | bytes 2359296 | tf_op jit(solution)/shard_map/split | solution.py:13
  68.0 4.0 %all-to-all-start.1 = ((bf16[2,768,192]{2,0,1:T(2,128)(2,1)}), bf16[2,768,192]{2,0,1:T(2,128)(2,1)S(1)}, u32[]{:S(2)}, u32[]{:S(2)}) async-start(bf16[2,768,192]{2,0,1:T(2,128)(2,1)} %get-tuple-element.6), calls=%async_computation.1 | async-start | bytes 1572864 | tf_op jit(solution)/shard_map/all_to_all | solution.py:64
  72.6 9.7 %all-to-all-done.1 = bf16[2,768,192]{2,0,1:T(2,128)(2,1)S(1)} async-done(((bf16[2,768,192]{2,0,1:T(2,128)(2,1)}), bf16[2,768,192]{2,0,1:T(2,128)(2,1)S(1)}, u32[]{:S(2)}, u32[]{:S(2)}) %all-to-all-start.1) | async-done | bytes 589856 | tf_op jit(solution)/shard_map/all_to_all | solution.py:64
  82.3 1.6 %broadcast_in_dim.2 = bf16[4,2,768,192]{2,3,1,0:T(8,128)(2,1)} broadcast(bf16[2,768,192]{1,2,0:T(8,128)(2,1)S(1)} %copy.25), dimensions={1,2,3} | broadcast | bytes 2949120 | tf_op jit(solution)/shard_map/broadcast_in_dim | solution.py:23
  83.9 3.6 %all-to-all-start.2 = ((bf16[4,2,768,192]{2,3,1,0:T(8,128)(2,1)}), bf16[4,2,768,192]{2,3,1,0:T(8,128)(2,1)S(1)}, u32[]{:S(2)}, u32[]{:S(2)}) async-start(bf16[4,2,768,192]{2,3,1,0:T(8,128)(2,1)} %broadcast_in_dim.2), calls=%async_computation.2 | async-start | bytes 4718592 | tf_op jit(solution)/shard_map/all_to_all | solution.py:24
  87.6 2.6 %copy.38 = bf16[2,4,192,192]{3,1,2,0:T(4,128)(2,1)} copy(bf16[2,4,192,192]{3,0,2,1:T(2,128)(2,1)} %bitcast.61) | data formatting | bytes 1179648 | tf_op jit(solution)/shard_map/all_to_all | solution.py:64
  90.2 2.6 %all_to_all.43 = bf16[2,192,768]{2,1,0:T(8,128)(2,1)} reshape(bf16[2,192,4,192]{3,2,1,0:T(4,128)(2,1)} %bitcast.62) | data formatting | bytes 1179648 | tf_op jit(solution)/shard_map/all_to_all | solution.py:64
  92.8 21.0 %all-to-all-done.2 = bf16[4,2,768,192]{2,3,1,0:T(8,128)(2,1)S(1)} async-done(((bf16[4,2,768,192]{2,3,1,0:T(8,128)(2,1)}), bf16[4,2,768,192]{2,3,1,0:T(8,128)(2,1)S(1)}, u32[]{:S(2)}, u32[]{:S(2)}) %all-to-all-start.2) | async-done | bytes 2359328 | tf_op jit(solution)/shard_map/all_to_all | solution.py:24
  115.6 1.8 %copy.28 = bf16[192,2,768]{0,1,2:T(2,128)(2,1)} copy(bf16[192,2,768]{2,0,1:T(8,128)(2,1)S(1)} %fusion.17) | data formatting | bytes 1179648 | tf_op jit(solution)/shard_map/convert_element_type | solution.py:71
  117.4 11.1 %all-to-all-start.3 = ((bf16[192,2,768]{0,1,2:T(2,128)(2,1)}), bf16[192,2,768]{0,1,2:T(2,128)(2,1)S(1)}, u32[]{:S(2)}, u32[]{:S(2)}) async-start(bf16[192,2,768]{0,1,2:T(2,128)(2,1)} %copy.28), calls=%async_computation.3 | async-start | bytes 1572864 | tf_op jit(solution)/shard_map/all_to_all | solution.py:72
  128.5 1.9 %fusion.13 = f32[12,192,128]{2,1,0:T(8,128)} fusion(bf16[128,128]{1,0:T(8,128)(2,1)S(1)} %copy-done.8, bf16[12,192,128]{2,1,0:T(8,128)(2,1)S(1)} %copy-done.1, f32[12,192]{1,0:T(8,128)S(1)} %add_rsqrt_fusion.1, f32[12,192]{1,0:T(8,128)S(1)} %broadcast_multiply_fusion.1), kind=kOutput, calls=%fused_computation.24 | convolution fusion | flops 77561856 | bytes 1820672 | tf_op jit(solution)/shard_map/ijd,de->ije/dot_general | solution.py:76
  130.4 21.0 %all-to-all-done.3 = bf16[192,2,768]{0,1,2:T(2,128)(2,1)S(1)} async-done(((bf16[192,2,768]{0,1,2:T(2,128)(2,1)}), bf16[192,2,768]{0,1,2:T(2,128)(2,1)S(1)}, u32[]{:S(2)}, u32[]{:S(2)}) %all-to-all-start.3) | async-done | bytes 589856 | tf_op jit(solution)/shard_map/all_to_all | solution.py:72
  152.8 1.1 multiply_reduce_fusion
  154.7 1.1 reshape.73
  155.8 2.5 %fusion.14 = bf16[12,192,128]{2,1,0:T(8,128)(2,1)} fusion(f32[12,192,128]{2,1,0:T(8,128)} %fusion.13, f32[192,128,12]{0,1,2:T(8,128)S(1)} %reshape.73, f32[192,12]{0,1:T(8,128)S(1)} %add_rsqrt_fusion, f32[192,12]{0,1:T(8,128)S(1)} %broadcast_multiply_fusion, bf16[128,128]{1,0:T(8,128)(2,1)S(1)} %copy-done.6), kind=kOutput, calls=%fused_computation.25 | convolution fusion | flops 76972032 | bytes 3000320 | tf_op jit(solution)/shard_map/jci,ce->ije/dot_general | solution.py:74
  (34 shorter events, 5.6 us)
Async XLA Ops:
  0.0 3.4 %copy-start = (bf16[128,128]{1,0:T(8,128)(2,1)S(1)}, bf16[128,128]{1,0:T(8,128)(2,1)}, u32[]{:S(2)}) copy-start(bf16[128,128]{1,0:T(8,128)(2,1)} %param.12) | copy-start | bytes 98308
  0.0 3.4 %copy-start.1 = (bf16[12,192,128]{2,1,0:T(8,128)(2,1)S(1)}, bf16[12,192,128]{2,1,0:T(8,128)(2,1)}, u32[]{:S(2)}) copy-start(bf16[12,192,128]{2,1,0:T(8,128)(2,1)} %param.8) | copy-start | bytes 1769476
  3.4 1.5 copy-start.7
  4.9 1.5 copy-start.9
  4.9 1.8 %copy-start.4 = (bf16[128,128]{1,0:T(8,128)(2,1)S(1)}, bf16[128,128]{1,0:T(8,128)(2,1)}, u32[]{:S(2)}) copy-start(bf16[128,128]{1,0:T(8,128)(2,1)} %param.13) | copy-start | bytes 98308
  6.8 1.3 copy-start.5
  68.0 14.3 %all-to-all-start.1 = ((bf16[2,768,192]{2,0,1:T(2,128)(2,1)}), bf16[2,768,192]{2,0,1:T(2,128)(2,1)S(1)}, u32[]{:S(2)}, u32[]{:S(2)}) async-start(bf16[2,768,192]{2,0,1:T(2,128)(2,1)} %get-tuple-element.6), calls=%async_computation.1 | async-start | bytes 1572864 | tf_op jit(solution)/shard_map/all_to_all | solution.py:64
  82.3 1.6 %copy-start.2 = (bf16[2,768,192]{2,0,1:T(2,128)(2,1)}, bf16[2,768,192]{2,0,1:T(2,128)(2,1)S(1)}, u32[]{:S(2)}) copy-start(bf16[2,768,192]{2,0,1:T(2,128)(2,1)S(1)} %all-to-all-done.1) | copy-start | bytes 1769476
  83.9 29.9 %all-to-all-start.2 = ((bf16[4,2,768,192]{2,3,1,0:T(8,128)(2,1)}), bf16[4,2,768,192]{2,3,1,0:T(8,128)(2,1)S(1)}, u32[]{:S(2)}, u32[]{:S(2)}) async-start(bf16[4,2,768,192]{2,3,1,0:T(8,128)(2,1)} %broadcast_in_dim.2), calls=%async_computation.2 | async-start | bytes 4718592 | tf_op jit(solution)/shard_map/all_to_all | solution.py:24
  113.9 1.1 copy-start.3
  115.6 12.9 %copy-start.8 = (bf16[128,128]{1,0:T(8,128)(2,1)S(1)}, bf16[128,128]{1,0:T(8,128)(2,1)}, u32[]{:S(2)}) copy-start(bf16[128,128]{1,0:T(8,128)(2,1)} %param.14) | copy-start | bytes 98308
  117.4 34.1 %all-to-all-start.3 = ((bf16[192,2,768]{0,1,2:T(2,128)(2,1)}), bf16[192,2,768]{0,1,2:T(2,128)(2,1)S(1)}, u32[]{:S(2)}, u32[]{:S(2)}) async-start(bf16[192,2,768]{0,1,2:T(2,128)(2,1)} %copy.28), calls=%async_computation.3 | async-start | bytes 1572864 | tf_op jit(solution)/shard_map/all_to_all | solution.py:72
  154.7 1.1 copy-start.6
where the time goes:
time: 159 us; the launch traced here: 158 us
  blocking collectives  52 us (33%)
  waiting for transfers between devices  51.8 us (33%)
  starting transfers between devices  18.7 us (12%)
  local copies, waits for them, and re-layouts  17.8 us (11%)
  matrix products  10.9 us (7%)
  other arithmetic  6.88 us (4%)
    all_to_all x1, blocking collectives, in_one_piece(): lax.all_to_all(both, axis, split_axis=split_dim, concat_axis=concat_dim,...  52 us
    all_to_all x1, waiting for transfers between devices, local(): lax.all_to_all(triangle, 'row', split_axis=2, concat_axis=1, tiled=True)  21 us
    all_to_all x1, waiting for transfers between devices, copy_for_each(): return lax.all_to_all(copies, axis, split_axis=0, concat_axis=0, tiled=True)  21 us
    all_to_all x1, starting transfers between devices, local(): lax.all_to_all(triangle, 'row', split_axis=2, concat_axis=1, tiled=True)  11.1 us
    all_to_all x1, waiting for transfers between devices, local(): lax.all_to_all(right_rows, 'col', split_axis=1, concat_axis=2, tiled=True)  9.73 us
    dot_general x4, matrix products, project(): jnp.einsum('ijd,de->eij', normed, weight, preferred_element_type=jnp.floa...  5.51 us
    all_to_all x2, local copies, waits for them, and re-layouts, local(): lax.all_to_all(right_rows, 'col', split_axis=1, concat_axis=2, tiled=True)  5.25 us
    all_to_all x1, starting transfers between devices, local(): lax.all_to_all(right_rows, 'col', split_axis=1, concat_axis=2, tiled=True)  4.01 us
  transfers between devices with their start and end apart: 3, of which 3 were waited for; matrix products, arithmetic and copies ran while one was open for 3% of the time, Pallas kernels for 0%

commit v1 on v0

v1 whole, which is shorter than its diff:
```python
import functools

import jax
import jax.numpy as jnp
from jax import lax
from jax.experimental import pallas as pl
from jax.experimental.pallas import tpu as pltpu
from jax.sharding import PartitionSpec as P

MESH = pl.DeviceIdType.MESH
NX, NY, NZ, NS, NC = 4, 4, 8, 32, 128
ROWS, COLS, WIDTH = 12, 192, 128
F32, BF16 = jnp.float32, jnp.bfloat16


def unit_norm(values, axis):
    mean = jnp.mean(values, axis=axis, keepdims=True)
    centred = values - mean
    spread = jnp.mean(centred * centred, axis=axis, keepdims=True)
    return centred * lax.rsqrt(spread + 1e-05)


def kernel(
    x_ref, tm_ref, wlg_ref, wl_ref, wrg_ref, wr_ref, wog_ref, wo_ref, out_ref,
    wt, normed, gate, stage, msg, r_own, r_all, l_own, t_odd, t_a, t_b, t_in,
    send_sem, r_sem, l_sem, t_sem, swap_sem, swap_send, local_sem, line_y, line_z,
):
    row, q = lax.axis_index("row"), lax.axis_index("col")
    core, y, z = row % 2, (row // 2) % NY, row // (2 * NY)
    s = row // 2
    chip = s * NX + q
    other = ((s * 2) + 1 - core, q)

    def at(zz, yy, xx):
        return ((zz * NY + yy) * 2 + core, xx)

    x_line = [at(z, y, (q + d) % NX) for d in range(1, NX)]
    y_line = [at(z, (y + d) % NY, q) for d in range(1, NY)]
    z_line = [at((z + d) % NZ, y, q) for d in range(1, NZ)]
    barrier = pltpu.get_barrier_semaphore()
    for peer in [other, *x_line, *y_line, *z_line]:
        pl.semaphore_signal(barrier, inc=1, device_id=peer, device_id_type=MESH)

    for n, w in enumerate((wlg_ref, wl_ref, wrg_ref, wr_ref)):
        wt[n * WIDTH : (n + 1) * WIDTH, :] = w[...].astype(F32).T.astype(BF16)
    low = lax.broadcasted_iota(jnp.int32, (WIDTH, 128), 1) < 64
    odd_q = q % 2 == 1

    def pair_of_rows(p, _):
        parts = {}
        for e in range(2):
            i = 2 * p + e
            n = unit_norm(x_ref[i].astype(F32), 1)
            normed[i] = n.astype(BF16)
            tile = (row * ROWS + i) // 64
            for t in range(3):
                m = tm_ref[tile, q * 3 + t].astype(F32)
                parts[e, t] = (n[t * 64 : (t + 1) * 64] * m).astype(BF16)
        rhs = jnp.concatenate(
            [parts[0, 0], parts[0, 1], parts[1, 0], parts[1, 1], parts[0, 2], parts[1, 2]], axis=0
        )

        def project(n):
            return lax.dot_general(
                wt[n * WIDTH : (n + 1) * WIDTH, :], rhs, (((1,), (1,)), ((), ())),
                preferred_element_type=F32,
            )

        left = jax.nn.sigmoid(project(0)) * project(1)
        right = jax.nn.sigmoid(project(2)) * project(3)
        first = jnp.where(odd_q, right[:, 256:], left[:, 256:])
        second = jnp.where(odd_q, left[:, 256:], right[:, 256:])
        mixed = (
            jnp.where(low, first, pltpu.roll(second, 64, 1)),
            jnp.where(low, pltpu.roll(first, 64, 1), second),
        )
        for e in range(2):
            lanes = slice(e * 128, (e + 1) * 128)
            i = 2 * p + e
            stage[pl.ds(i, NC, stride=36), :] = right[:, lanes]
            stage[pl.ds(12 + i, NC, stride=36), :] = mixed[e]
            stage[pl.ds(24 + i, NC, stride=36), :] = left[:, lanes]
        return 0

    lax.fori_loop(0, ROWS // 2, pair_of_rows, 0)
    flat = msg.reshape(NC * 36, 128)

    def pack(n, _):
        rows = pl.ds(pl.multiple_of(n * 288, 288), 288)
        flat[rows, :] = stage[rows, :].astype(BF16)
        return 0

    lax.fori_loop(0, 16, pack, 0)

    pl.semaphore_wait(barrier, 1 + 3 + 3 + 7)
    for peer in y_line:
        pl.semaphore_signal(line_y, inc=1, device_id=peer, device_id_type=MESH)
    pl.semaphore_wait(line_y, 3)
    for peer in z_line:
        pl.semaphore_signal(line_z, inc=1, device_id=peer, device_id_type=MESH)
    pl.semaphore_wait(line_z, 7)

    def peer_of(o):
        dx, dy, dz = o % NX, (o // NX) % NY, (NZ // 2 + o // (NX * NY)) % NZ
        zz, yy, xx = (z + dz) % NZ, (y + dy) % NY, (q + dx) % NX
        return zz * NY + yy, xx

    me = 64

    def to_all(start):
        def body(o, _):
            start(*peer_of(o))
            return 0

        lax.fori_loop(0, me, body, 0)
        lax.fori_loop(me + 1, NC, body, 0)

    def send_r(ss, xx):
        pltpu.make_async_remote_copy(
            msg.at[ss * NX + xx, pl.ds(0, 2)], r_own.at[:, q, s], send_sem, r_sem,
            device_id=(ss * 2 + core, xx), device_id_type=MESH,
        ).start()

    def send_l(ss, xx):
        pltpu.make_async_remote_copy(
            msg.at[ss * NX + xx, 2], l_own.at[q, s], send_sem, l_sem,
            device_id=(ss * 2 + core, xx), device_id_type=MESH,
        ).start()

    to_all(send_r)
    to_all(send_l)
    own_r = pltpu.make_async_copy(msg.at[chip, pl.ds(0, 2)], r_own.at[:, q, s], local_sem.at[0])
    own_l = pltpu.make_async_copy(msg.at[chip, 2], l_own.at[q, s], local_sem.at[1])
    own_r.start()
    own_l.start()

    def gates(i, _):
        gate[i] = jax.nn.sigmoid(
            jnp.dot(normed[i], wog_ref[...], preferred_element_type=F32)
        )
        return 0

    lax.fori_loop(0, ROWS, gates, 0)

    own_r.wait()
    own_l.wait()
    every = msg.at[pl.ds(0, NC - 1), pl.ds(0, 2)]
    pltpu.make_async_copy(every, every, r_sem).wait()
    swap = pltpu.make_async_remote_copy(
        r_own, r_all.at[:, :, :, core], swap_send, swap_sem, device_id=other, device_id_type=MESH
    )
    swap.start()
    keep = pltpu.make_async_copy(r_own, r_all.at[:, :, :, core], local_sem.at[2])
    keep.start()
    every = msg.at[pl.ds(0, NC - 1), 2]
    pltpu.make_async_copy(every, every, l_sem).wait()
    keep.wait()
    swap.wait()

    la = l_own.reshape(NX * 384, 128)
    ra = r_all.reshape(2 * NX * 768, 128)
    rb = r_own.reshape(2 * NX * 384, 128)

    def block(ref, n, size):
        return ref[n * size : (n + 1) * size, :]

    lhs = [block(la, x, 384) for x in range(NX)]
    rhs = [block(ra, x, 768) for x in range(NX)]
    for x in (0, 2):
        lhs.append(
            jnp.concatenate(
                [block(rb, NX + x, 384)[:, :64], block(rb, NX + x + 1, 384)[:, 64:]], axis=1
            )
        )
        rhs.append(
            jnp.concatenate(
                [block(ra, NX + x, 768)[:, 64:], block(ra, NX + x + 1, 768)[:, :64]], axis=1
            )
        )
    triangle = lax.dot_general(
        jnp.concatenate(lhs, axis=1), jnp.concatenate(rhs, axis=1), (((1,), (1,)), ((), ())),
        preferred_element_type=F32,
    )
    whole = t_a.reshape(NX * 384, 128)
    halves = t_b.reshape(NX * 192, 128)
    lane_b = lax.broadcasted_iota(jnp.int32, (192, 128), 1) < 64
    for x, tile in enumerate((0, 2, 3, 5)):
        whole[x * 384 : (x + 1) * 384, :] = triangle[:, tile * 128 : (tile + 1) * 128].astype(BF16)
    for n, tile in enumerate((1, 4)):
        t_odd[...] = triangle[:, tile * 128 : (tile + 1) * 128]
        even, odd = t_odd[pl.ds(0, 192, stride=2), :], t_odd[pl.ds(1, 192, stride=2), :]
        b0 = jnp.where(lane_b, even, pltpu.roll(odd, 64, 1))
        b1 = jnp.where(lane_b, pltpu.roll(even, 64, 1), odd)
        halves[(2 * n) * 192 : (2 * n + 1) * 192, :] = b0.astype(BF16)
        halves[(2 * n + 1) * 192 : (2 * n + 2) * 192, :] = b1.astype(BF16)

    def send_t(ss, xx):
        for src, dst in ((t_a, pl.ds(0, 6)), (t_b, pl.ds(6, 3))):
            pltpu.make_async_remote_copy(
                src.at[xx, ss], t_in.at[chip, dst], send_sem, t_sem,
                device_id=(ss * 2 + core, xx), device_id_type=MESH,
            ).start()

    to_all(send_t)
    own_a = pltpu.make_async_copy(t_a.at[q, s], t_in.at[chip, pl.ds(0, 6)], local_sem.at[0])
    own_b = pltpu.make_async_copy(t_b.at[q, s], t_in.at[chip, pl.ds(6, 3)], local_sem.at[1])
    own_a.start()
    own_b.start()
    own_a.wait()
    own_b.wait()
    every = t_in.at[pl.ds(0, NC - 1)]
    pltpu.make_async_copy(every, every, t_sem).wait()

    flat_t = t_in.reshape(NC * 18, 128)

    def unpack(n, _):
        rows = pl.ds(pl.multiple_of(n * 288, 288), 288)
        stage[rows, :] = flat_t[rows, :].astype(F32)
        return 0

    lax.fori_loop(0, 8, unpack, 0)

    def projected(g):
        scaled = unit_norm(stage[pl.ds(g, NC, stride=18), :], 0)
        return jnp.dot(scaled.T.astype(BF16), wo_ref[...], preferred_element_type=F32)

    a0 = pl.multiple_of((q % 2) * 64, 64)
    b0 = pl.multiple_of((1 - q % 2) * 128, 128)

    def whole_rows(i, _):
        out_ref[i, pl.ds(a0, 128), :] = (gate[i, pl.ds(a0, 128), :] * projected(i)).astype(BF16)
        return 0

    def half_rows(p, _):
        both = projected(12 + p)
        for e in range(2):
            out_ref[2 * p + e, pl.ds(b0, 64), :] = (
                gate[2 * p + e, pl.ds(b0, 64), :] * both[e * 64 : (e + 1) * 64]
            ).astype(BF16)
        return 0

    lax.fori_loop(0, 12, whole_rows, 0)
    lax.fori_loop(0, 6, half_rows, 0)
    sent = msg.at[pl.ds(0, NC - 1)]
    pltpu.make_async_copy(sent, sent, send_sem).wait()
    sent = t_in.at[pl.ds(0, NC - 1)]
    pltpu.make_async_copy(sent, sent, send_sem).wait()


def local(*args):
    vmem = pl.BlockSpec(memory_space=pltpu.VMEM)
    smem = pl.BlockSpec(memory_space=pltpu.SMEM)
    dma = pltpu.SemaphoreType.DMA
    return pl.pallas_call(
        kernel,
        out_shape=jax.ShapeDtypeStruct((ROWS, COLS, WIDTH), BF16),
        in_specs=[vmem, smem] + [vmem] * 6,
        out_specs=vmem,
        scratch_shapes=[
            pltpu.VMEM((4 * WIDTH, WIDTH), BF16),
            pltpu.VMEM((ROWS, COLS, WIDTH), BF16),
            pltpu.VMEM((ROWS, COLS, WIDTH), F32),
            pltpu.VMEM((NC * 36, 128), F32),
            pltpu.VMEM((NC, 3, 3, 4, 128), BF16),
            pltpu.VMEM((2, NX, NS, 3, 4, 128), BF16),
            pltpu.VMEM((2, NX, NS, 2, 3, 4, 128), BF16),
            pltpu.VMEM((NX, NS, 3, 4, 128), BF16),
            pltpu.VMEM((384, 128), F32),
            pltpu.VMEM((NX, NS, 6, 2, 128), BF16),
            pltpu.VMEM((NX, NS, 3, 2, 128), BF16),
            pltpu.VMEM((NC, 9, 2, 128), BF16),
            dma, dma, dma, dma, dma, dma, pltpu.SemaphoreType.DMA((3,)),
            pltpu.SemaphoreType.REGULAR, pltpu.SemaphoreType.REGULAR,
        ],
        compiler_params=pltpu.CompilerParams(
            collective_id=0, has_side_effects=True, vmem_limit_bytes=48 * 2**20
        ),
    )(*args)


def solution(mesh):
    return jax.shard_map(
        local,
        mesh=mesh,
        in_specs=(P("row", "col", None), P(), P(), P(), P(), P(), P(), P()),
        out_specs=P("row", "col", None),
        check_vma=False,
    )
```

time: 159 us -> 77.4 us (0.49)
  the two profiles are of different devices: /device:TPU:1 before, /device:TPU:32 now
where the time goes in v1:
time: 77.4 us; the launch traced here: 76.8 us
  Pallas kernels  69.7 us (90%)
  local copies, waits for them, and re-layouts  7.12 us (9%)
    pallas_call x1, Pallas kernels, local(): pl.pallas_call(kernel, out_shape=jax.ShapeDtypeStruct((ROWS, COLS, WIDTH)...  69.7 us
    unnamed x17, local copies, waits for them, and re-layouts  7.12 us

profile of v1, /device:TPU:32, one launch (start us, length us, event | category | flops | bytes accessed | tf_op | source)
XLA Modules:
  0.0 76.8 jit_solution(10907119654879202524)
XLA Ops:
  0.0 0.0 copy-start
  0.0 1.1 %copy-done = bf16[12,192,128]{2,1,0:T(8,128)(2,1)S(1)} copy-done((bf16[12,192,128]{2,1,0:T(8,128)(2,1)S(1)}, bf16[12,192,128]{2,1,0:T(8,128)(2,1)}, u32[]{:S(2)}) %copy-start) | copy-done | bytes 589848
  1.1 0.0 copy-start.1
  1.1 0.8 copy-done.1
  1.8 0.0 copy-start.2
  1.8 0.8 copy-done.2
  2.6 0.0 copy-start.3
  2.6 0.8 copy-done.3
  3.3 0.0 copy-start.4
  3.3 0.8 copy-done.4
  4.1 0.0 copy-start.5
  4.1 0.8 copy-done.5
  4.9 0.0 copy-start.6
  4.9 0.8 copy-done.6
  5.6 0.0 copy-start.7
  5.6 0.7 copy-done.7
  6.3 69.7 %shard_map.82 = bf16[12,192,128]{2,1,0:T(8,128)(2,1)S(1)} custom-call(bf16[12,192,128]{2,1,0:T(8,128)(2,1)S(1)} %copy-done, s32[12,12]{1,0:T(8,128)S(1)} %copy-done.7, bf16[128,128]{1,0:T(8,128)(2,1)S(1)} %copy-done.1, bf16[128,128]{1,0:T(8,128)(2,1)S(1)} %copy-done.2, bf16[128,128]{1,0:T(8,128)(2,1)S(1)} %copy-done.3, bf16[128,128]{1,0:T(8,128)(2,1)S(1)} %copy-done.4, ...), custom_call_target="tpu_custom_call" | custom-call | tf_op jit(solution)/shard_map/pallas_call | solution.py:254
  76.0 0.8 %copy.10 = bf16[12,192,128]{2,1,0:T(8,128)(2,1)} copy(bf16[12,192,128]{2,1,0:T(8,128)(2,1)S(1)} %shard_map.82) | data formatting | bytes 1179648
Async XLA Ops:
  0.0 1.1 %copy-start = (bf16[12,192,128]{2,1,0:T(8,128)(2,1)S(1)}, bf16[12,192,128]{2,1,0:T(8,128)(2,1)}, u32[]{:S(2)}) copy-start(bf16[12,192,128]{2,1,0:T(8,128)(2,1)} %x_ref.1) | copy-start | bytes 1769476
  1.1 0.8 copy-start.1
  1.8 0.8 copy-start.2
  2.6 0.8 copy-start.3
  3.3 0.8 copy-start.4
  4.1 0.8 copy-start.5
  4.9 0.8 copy-start.6
  5.6 0.7 copy-start.7

commit v2 on v1

v2 whole, which is shorter than its diff:
```python
import functools

import jax
import jax.numpy as jnp
from jax import lax
from jax.experimental import pallas as pl
from jax.experimental.pallas import tpu as pltpu
from jax.sharding import PartitionSpec as P

MESH = pl.DeviceIdType.MESH
NX, NY, NZ, NS, NC = 4, 4, 8, 32, 128
ROWS, COLS, WIDTH = 12, 192, 128
F32, BF16 = jnp.float32, jnp.bfloat16
UNROLL = 3


def unit_norm(values, axis):
    mean = jnp.mean(values, axis=axis, keepdims=True)
    centred = values - mean
    spread = jnp.mean(centred * centred, axis=axis, keepdims=True)
    return centred * lax.rsqrt(spread + 1e-05)


def kernel(
    x_hbm, tm_hbm, wlg_hbm, wl_hbm, wrg_hbm, wr_hbm, wog_hbm, wo_hbm, out_ref,
    x_ref, tm_ref, w_in, wt, normed, gate, stage, msg, r_own, r_all, r_mix, l_own, t_odd, t_a, t_b,
    in_a, in_b, load_sem, send_sem, r_sem, l_sem, a_sem, b_sem, swap_sem, swap_send, keep_sem,
    line_y, line_x,
):
    row, q = lax.axis_index("row"), lax.axis_index("col")
    core, y, z = row % 2, (row // 2) % NY, row // (2 * NY)
    s = row // 2
    chip = s * NX + q
    other = ((s * 2) + 1 - core, q)

    loads = [
        [
            pltpu.make_async_copy(w, w_in.at[n], load_sem.at[0])
            for n, w in enumerate((wlg_hbm, wl_hbm, wrg_hbm, wr_hbm, wog_hbm, wo_hbm))
        ],
        [pltpu.make_async_copy(tm_hbm, tm_ref, load_sem.at[1])],
    ] + [
        [pltpu.make_async_copy(x_hbm.at[pl.ds(4 * n, 4)], x_ref.at[pl.ds(4 * n, 4)], load_sem.at[2 + n])]
        for n in range(3)
    ]
    for load in loads:
        for copy in load:
            copy.start()

    def at(zz, yy, xx):
        return ((zz * NY + yy) * 2 + core, xx)

    x_line = [at(z, y, (q + d) % NX) for d in range(1, NX)]
    y_line = [at(z, (y + d) % NY, q) for d in range(1, NY)]
    z_line = [at((z + d) % NZ, y, q) for d in range(1, NZ)]
    barrier = pltpu.get_barrier_semaphore()
    for peer in [*z_line, other, *x_line, *y_line]:
        pl.semaphore_signal(barrier, inc=1, device_id=peer, device_id_type=MESH)

    pltpu.make_async_copy(w_in, w_in, load_sem.at[0]).wait()
    for n in range(4):
        wt[n * WIDTH : (n + 1) * WIDTH, :] = w_in[n].astype(F32).T.astype(BF16)
    low = lax.broadcasted_iota(jnp.int32, (WIDTH, 128), 1) < 64
    odd_q = q % 2 == 1
    loads[1][0].wait()

    def pair_of_rows(p, _):
        parts = {}
        for e in range(2):
            i = 2 * p + e
            n = unit_norm(x_ref[i].astype(F32), 1)
            normed[i] = n.astype(BF16)
            tile = (row * ROWS + i) // 64
            for t in range(3):
                m = tm_ref[tile, q * 3 + t].astype(F32)
                parts[e, t] = (n[t * 64 : (t + 1) * 64] * m).astype(BF16)
        rhs = jnp.concatenate(
            [parts[0, 0], parts[0, 1], parts[1, 0], parts[1, 1], parts[0, 2], parts[1, 2]], axis=0
        )

        def project(n):
            return lax.dot_general(
                wt[n * WIDTH : (n + 1) * WIDTH, :], rhs, (((1,), (1,)), ((), ())),
                preferred_element_type=F32,
            )

        left = jax.nn.sigmoid(project(0)) * project(1)
        right = jax.nn.sigmoid(project(2)) * project(3)
        first = jnp.where(odd_q, right[:, 256:], left[:, 256:])
        second = jnp.where(odd_q, left[:, 256:], right[:, 256:])
        mixed = (
            jnp.where(low, first, pltpu.roll(second, 64, 1)),
            jnp.where(low, pltpu.roll(first, 64, 1), second),
        )
        for e in range(2):
            lanes = slice(e * 128, (e + 1) * 128)
            i = 2 * p + e
            stage[pl.ds(i, NC, stride=36), :] = right[:, lanes]
            stage[pl.ds(12 + i, NC, stride=36), :] = mixed[e]
            stage[pl.ds(24 + i, NC, stride=36), :] = left[:, lanes]
        return 0

    loads[2][0].wait()
    lax.fori_loop(0, 2, pair_of_rows, 0)
    pl.semaphore_wait(barrier, 1 + 3 + 3 + 7)
    for peer in y_line:
        pl.semaphore_signal(line_y, inc=1, device_id=peer, device_id_type=MESH)
    loads[3][0].wait()
    lax.fori_loop(2, 4, pair_of_rows, 0)
    pl.semaphore_wait(line_y, 3)
    for peer in x_line:
        pl.semaphore_signal(line_x, inc=1, device_id=peer, device_id_type=MESH)
    loads[4][0].wait()
    lax.fori_loop(4, 6, pair_of_rows, 0)
    flat = msg.reshape(NC * 36, 128)

    def pack(n, _):
        rows = pl.ds(pl.multiple_of(n * 288, 288), 288)
        flat[rows, :] = stage[rows, :].astype(BF16)
        return 0

    lax.fori_loop(0, 16, pack, 0)
    pl.semaphore_wait(line_x, 3)

    def to_group(k):
        return (z + NZ // 2 + k) % NZ

    def from_group(k):
        return (z + NZ // 2 - k) % NZ

    me = 64

    def to_all(begin, send):
        def one(o, _):
            k = o // 16
            send(k, to_group(k) * NY + (y + (o // NX)) % NY, (q + o) % NX)
            return 0

        lax.fori_loop(begin, me, one, 0)
        lax.fori_loop(me + 1, NC, one, 0)

    def send_r(k, ss, xx):
        pltpu.make_async_remote_copy(
            msg.at[ss * NX + xx, pl.ds(0, 2)], r_own.at[:, q, s], send_sem, r_sem.at[k],
            device_id=(ss * 2 + core, xx), device_id_type=MESH,
        ).start()

    def send_l(k, ss, xx):
        pltpu.make_async_remote_copy(
            msg.at[ss * NX + xx, 2], l_own.at[q, s], send_sem, l_sem.at[k],
            device_id=(ss * 2 + core, xx), device_id_type=MESH,
        ).start()

    pltpu.make_async_copy(msg.at[chip, pl.ds(0, 2)], r_own.at[:, q, s], r_sem.at[4]).start()
    pltpu.make_async_copy(msg.at[chip, 2], l_own.at[q, s], l_sem.at[4]).start()
    to_all(0, send_r)
    to_all(0, send_l)

    def gates(i, _):
        gate[i] = jax.nn.sigmoid(jnp.dot(normed[i], w_in[4], preferred_element_type=F32))
        return 0

    lax.fori_loop(0, ROWS, gates, 0)

    def swap(k, _):
        four = pl.ds(from_group(k) * NY, NY)
        block = r_own.at[:, :, four]
        pltpu.make_async_copy(block, block, r_sem.at[k]).wait()
        pltpu.make_async_remote_copy(
            block, r_all.at[:, :, four, core], swap_send, swap_sem, device_id=other, device_id_type=MESH
        ).start()
        pltpu.make_async_copy(block, r_all.at[:, :, four, core], keep_sem).start()
        return 0

    lax.fori_loop(0, NZ, swap, 0)
    pltpu.make_async_copy(r_own, r_own, keep_sem).wait()
    pltpu.make_async_copy(r_own, r_own, swap_sem).wait()

    ra = r_all.reshape(2 * NX * 768, 128)
    rb = r_own.reshape(2 * NX * 384, 128)
    la = l_own.reshape(NX * 384, 128)
    whole = t_a.reshape(NX * 384, 128)
    halves = t_b.reshape(NX * 192, 128)

    def block(ref, n, size):
        return ref[n * size : (n + 1) * size, :]

    for n, x in enumerate((0, 2)):
        r_mix[n] = jnp.concatenate(
            [block(ra, NX + x, 768)[:, 64:], block(ra, NX + x + 1, 768)[:, :64]], axis=1
        )
    lane_b = lax.broadcasted_iota(jnp.int32, (24, 128), 1) < 64

    def rows_of(k, _):
        zz = from_group(k)
        arrived = msg.at[pl.ds(0, 16), 2]
        pltpu.make_async_copy(arrived, arrived, l_sem.at[k]).wait()

        def part(ref, n):
            return ref[pl.ds(pl.multiple_of(n * 384 + zz * 48, 48), 48), :]

        lhs = [part(la, x) for x in range(NX)]
        for x in (0, 2):
            lhs.append(
                jnp.concatenate([part(rb, NX + x)[:, :64], part(rb, NX + x + 1)[:, 64:]], axis=1)
            )
        rhs = [block(ra, x, 768) for x in range(NX)] + [r_mix[0], r_mix[1]]
        triangle = lax.dot_general(
            jnp.concatenate(lhs, axis=1), jnp.concatenate(rhs, axis=1), (((1,), (1,)), ((), ())),
            preferred_element_type=F32,
        )
        for x, tile in enumerate((0, 2, 3, 5)):
            whole[pl.ds(pl.multiple_of(x * 384 + zz * 48, 48), 48), :] = triangle[
                :, tile * 128 : (tile + 1) * 128
            ].astype(BF16)
        for n, tile in enumerate((1, 4)):
            t_odd[n] = triangle[:, tile * 128 : (tile + 1) * 128]
            even, odd = t_odd[n, pl.ds(0, 24, stride=2), :], t_odd[n, pl.ds(1, 24, stride=2), :]
            b0 = jnp.where(lane_b, even, pltpu.roll(odd, 64, 1))
            b1 = jnp.where(lane_b, pltpu.roll(even, 64, 1), odd)
            halves[pl.ds(pl.multiple_of(2 * n * 192 + zz * 24, 8), 24), :] = b0.astype(BF16)
            halves[pl.ds(pl.multiple_of((2 * n + 1) * 192 + zz * 24, 8), 24), :] = b1.astype(BF16)

        def back(j, _):
            ss, xx = zz * NY + (y + j // NX) % NY, (q + j) % NX

            @pl.when((k != 4) | (j != 0))
            def _():
                pltpu.make_async_remote_copy(
                    t_a.at[xx, ss], in_a.at[chip], send_sem, a_sem,
                    device_id=(ss * 2 + core, xx), device_id_type=MESH,
                ).start()

            return 0

        lax.fori_loop(0, 16, back, 0)
        return 0

    lax.fori_loop(0, NZ, rows_of, 0)
    pltpu.make_async_copy(t_a.at[q, s], in_a.at[chip], a_sem).start()
    pltpu.make_async_copy(t_b.at[q, s], in_b.at[chip], b_sem).start()

    def send_b(k, ss, xx):
        pltpu.make_async_remote_copy(
            t_b.at[xx, ss], in_b.at[chip], send_sem, b_sem,
            device_id=(ss * 2 + core, xx), device_id_type=MESH,
        ).start()

    to_all(0, send_b)

    def unpack(source, steps):
        def some(n, _):
            rows = pl.ds(pl.multiple_of(n * 256, 256), 256)
            stage[rows, :] = source[rows, :].astype(F32)
            return 0

        lax.fori_loop(0, steps, some, 0)

    def projected(g, stride):
        scaled = unit_norm(stage[pl.ds(g, NC, stride=stride), :], 0)
        return jnp.dot(scaled.T.astype(BF16), w_in[5], preferred_element_type=F32)

    a0 = pl.multiple_of((q % 2) * 64, 64)
    b0 = pl.multiple_of((1 - q % 2) * 128, 128)

    def whole_rows(i, _):
        out_ref[i, pl.ds(a0, 128), :] = (gate[i, pl.ds(a0, 128), :] * projected(i, 12)).astype(BF16)
        return 0

    def half_rows(p, _):
        both = projected(p, 6)
        for e in range(2):
            out_ref[2 * p + e, pl.ds(b0, 64), :] = (
                gate[2 * p + e, pl.ds(b0, 64), :] * both[e * 64 : (e + 1) * 64]
            ).astype(BF16)
        return 0

    pltpu.make_async_copy(in_a, in_a, a_sem).wait()
    unpack(in_a.reshape(NC * 12, 128), 6)
    lax.fori_loop(0, 12, whole_rows, 0, unroll=UNROLL)
    pltpu.make_async_copy(in_b, in_b, b_sem).wait()
    unpack(in_b.reshape(NC * 6, 128), 3)
    lax.fori_loop(0, 6, half_rows, 0, unroll=UNROLL)
    for sent in (msg, in_a, in_b):
        sent = sent.at[pl.ds(0, NC - 1)]
        pltpu.make_async_copy(sent, sent, send_sem).wait()
    pltpu.make_async_copy(r_own, r_own, swap_send).wait()


def local(*args):
    hbm = pl.BlockSpec(memory_space=pltpu.HBM)
    vmem = pl.BlockSpec(memory_space=pltpu.VMEM)
    dma = pltpu.SemaphoreType.DMA
    return pl.pallas_call(
        kernel,
        out_shape=jax.ShapeDtypeStruct((ROWS, COLS, WIDTH), BF16),
        in_specs=[hbm] * 8,
        out_specs=vmem,
        scratch_shapes=[
            pltpu.VMEM((ROWS, COLS, WIDTH), BF16),
            pltpu.SMEM((12, 12), jnp.int32),
            pltpu.VMEM((6, WIDTH, WIDTH), BF16),
            pltpu.VMEM((4 * WIDTH, WIDTH), BF16),
            pltpu.VMEM((ROWS, COLS, WIDTH), BF16),
            pltpu.VMEM((ROWS, COLS, WIDTH), F32),
            pltpu.VMEM((NC * 36, 128), F32),
            pltpu.VMEM((NC, 3, 3, 4, 128), BF16),
            pltpu.VMEM((2, NX, NS, 3, 4, 128), BF16),
            pltpu.VMEM((2, NX, NS, 2, 3, 4, 128), BF16),
            pltpu.VMEM((2, 768, 128), BF16),
            pltpu.VMEM((NX, NS, 3, 4, 128), BF16),
            pltpu.VMEM((2, 48, 128), F32),
            pltpu.VMEM((NX, NS, 6, 2, 128), BF16),
            pltpu.VMEM((NX, NS, 3, 2, 128), BF16),
            pltpu.VMEM((NC, 6, 2, 128), BF16),
            pltpu.VMEM((NC, 3, 2, 128), BF16),
            dma((5,)), dma, dma((NZ,)), dma((NZ,)), dma, dma, dma, dma, dma,
            pltpu.SemaphoreType.REGULAR, pltpu.SemaphoreType.REGULAR,
        ],
        compiler_params=pltpu.CompilerParams(
            collective_id=0, has_side_effects=True, vmem_limit_bytes=67043328
        ),
    )(*args)


def solution(mesh):
    return jax.shard_map(
        local,
        mesh=mesh,
        in_specs=(P("row", "col", None), P(), P(), P(), P(), P(), P(), P()),
        out_specs=P("row", "col", None),
        check_vma=False,
    )
```

time: 77.4 us -> 63.3 us (0.82)
  the two profiles are of different devices: /device:TPU:32 before, /device:TPU:1 now
where the time goes in v2:
time: 63.3 us; the launch traced here: 63.2 us
  Pallas kernels  61.2 us (97%)
  local copies, waits for them, and re-layouts  1.92 us (3%)
    pallas_call x1, Pallas kernels, local(): pl.pallas_call(kernel, out_shape=jax.ShapeDtypeStruct((ROWS, COLS, WIDTH)...  61.2 us
    unnamed x1, local copies, waits for them, and re-layouts  1.92 us

profile of v2, /device:TPU:1, one launch (start us, length us, event | category | flops | bytes accessed | tf_op | source)
XLA Modules:
  0.0 63.2 jit_solution(14938259926393183028)
XLA Ops:
  0.0 61.2 %shard_map.82 = bf16[12,192,128]{2,1,0:T(8,128)(2,1)} custom-call(bf16[12,192,128]{2,1,0:T(8,128)(2,1)} %x_hbm.1, s32[12,12]{1,0:T(8,128)} %tm_hbm.1, bf16[128,128]{1,0:T(8,128)(2,1)} %wlg_hbm.1, bf16[128,128]{1,0:T(8,128)(2,1)} %wl_hbm.1, bf16[128,128]{1,0:T(8,128)(2,1)} %wrg_hbm.1, bf16[128,128]{1,0:T(8,128)(2,1)} %wr_hbm.1, bf16[128,128]{1,0:T(8,128)(2,1)} %wog_hbm.1, ...), custom_call_target="tpu_custom_call" | custom-call | tf_op jit(solution)/shard_map/pallas_call | solution.py:294
  61.2 1.9 %copy.10 = bf16[12,192,128]{2,1,0:T(8,128)(2,1)} copy(bf16[12,192,128]{2,1,0:T(8,128)(2,1)} %shard_map.82) | data formatting | bytes 1179648

commit v3 on v2

v3 whole, which is shorter than its diff:
```python
import functools

import jax
import jax.numpy as jnp
from jax import lax
from jax.experimental import pallas as pl
from jax.experimental.pallas import tpu as pltpu
from jax.sharding import PartitionSpec as P

MESH = pl.DeviceIdType.MESH
NX, NY, NZ, NS, NC = 4, 4, 8, 32, 128
ROWS, COLS, WIDTH = 12, 192, 128
F32, BF16 = jnp.float32, jnp.bfloat16
UNROLL, UNROLL_PREP = 3, 3


def unit_norm(values, axis):
    mean = jnp.mean(values, axis=axis, keepdims=True)
    centred = values - mean
    spread = jnp.mean(centred * centred, axis=axis, keepdims=True)
    return centred * lax.rsqrt(spread + 1e-05)


def kernel(
    x_hbm, tm_hbm, wlg_hbm, wl_hbm, wrg_hbm, wr_hbm, wog_hbm, wo_hbm, out_ref,
    x_ref, tm_ref, w_in, wt, normed, masked, gate, stage, msg_r, msg_l, r_own, r_all, r_mix, l_own,
    t_odd, t_a, t_b, in_a, in_b,
    load_sem, send_sem, r_sem, l_sem, a_sem, b_sem, swap_sem, swap_send, keep_sem, line_y, line_x,
):
    row, q = lax.axis_index("row"), lax.axis_index("col")
    core, y, z = row % 2, (row // 2) % NY, row // (2 * NY)
    s = row // 2
    chip = s * NX + q
    other = ((s * 2) + 1 - core, q)

    weights = (wlg_hbm, wl_hbm, wrg_hbm, wr_hbm, wog_hbm, wo_hbm)
    for n, w in enumerate(weights):
        pltpu.make_async_copy(w, w_in.at[n], load_sem.at[0]).start()
    load_mask = pltpu.make_async_copy(tm_hbm, tm_ref, load_sem.at[1])
    load_mask.start()
    load_x = [
        pltpu.make_async_copy(x_hbm.at[pl.ds(6 * n, 6)], x_ref.at[pl.ds(6 * n, 6)], load_sem.at[2 + n])
        for n in range(2)
    ]
    for load in load_x:
        load.start()

    def at(zz, yy, xx):
        return ((zz * NY + yy) * 2 + core, xx)

    x_line = [at(z, y, (q + d) % NX) for d in range(1, NX)]
    y_line = [at(z, (y + d) % NY, q) for d in range(1, NY)]
    z_line = [at((z + d) % NZ, y, q) for d in (4, 3, 5, 2, 6, 1, 7)]
    barrier = pltpu.get_barrier_semaphore()
    for peer in [*z_line, *y_line, *x_line, other]:
        pl.semaphore_signal(barrier, inc=1, device_id=peer, device_id_type=MESH)

    pltpu.make_async_copy(w_in, w_in, load_sem.at[0]).wait()
    for n in range(4):
        wt[n * WIDTH : (n + 1) * WIDTH, :] = w_in[n].astype(F32).T.astype(BF16)
    low = lax.broadcasted_iota(jnp.int32, (WIDTH, 128), 1) < 64
    odd_q = q % 2 == 1
    load_mask.wait()

    def project(n, values):
        return lax.dot_general(
            wt[n * WIDTH : (n + 1) * WIDTH, :], values, (((1,), (1,)), ((), ())),
            preferred_element_type=F32,
        )

    def right_rows(p, _):
        parts = {}
        for e in range(2):
            i = 2 * p + e
            n = unit_norm(x_ref[i].astype(F32), 1)
            normed[i] = n.astype(BF16)
            tile = (row * ROWS + i) // 64
            for t in range(3):
                m = tm_ref[tile, q * 3 + t].astype(F32)
                parts[e, t] = (n[t * 64 : (t + 1) * 64] * m).astype(BF16)
        firsts = jnp.concatenate([parts[0, 0], parts[0, 1], parts[1, 0], parts[1, 1]], axis=0)
        lasts = jnp.concatenate([parts[0, 2], parts[1, 2]], axis=0)
        masked[p] = firsts
        right = jax.nn.sigmoid(project(2, firsts)) * project(3, firsts)
        right_last = jax.nn.sigmoid(project(2, lasts)) * project(3, lasts)
        left_last = jax.nn.sigmoid(project(0, lasts)) * project(1, lasts)
        first = jnp.where(odd_q, right_last, left_last)
        second = jnp.where(odd_q, left_last, right_last)
        mixed = (
            jnp.where(low, first, pltpu.roll(second, 64, 1)),
            jnp.where(low, pltpu.roll(first, 64, 1), second),
        )
        for e in range(2):
            stage[pl.ds(2 * p + e, NC, stride=24), :] = right[:, e * 128 : (e + 1) * 128]
            stage[pl.ds(12 + 2 * p + e, NC, stride=24), :] = mixed[e]
        return 0

    def left_rows(p, _):
        left = jax.nn.sigmoid(project(0, masked[p])) * project(1, masked[p])
        for e in range(2):
            stage[pl.ds(2 * p + e, NC, stride=12), :] = left[:, e * 128 : (e + 1) * 128]
        return 0

    def pack(target, steps):
        def some(n, _):
            rows = pl.ds(pl.multiple_of(n * 256, 256), 256)
            target[rows, :] = stage[rows, :].astype(BF16)
            return 0

        lax.fori_loop(0, steps, some, 0)

    load_x[0].wait()
    lax.fori_loop(0, 3, right_rows, 0, unroll=UNROLL_PREP)
    pl.semaphore_wait(barrier, 1 + 3 + 3 + 7)
    for peer in y_line:
        pl.semaphore_signal(line_y, inc=1, device_id=peer, device_id_type=MESH)
    load_x[1].wait()
    lax.fori_loop(3, 6, right_rows, 0, unroll=UNROLL_PREP)
    pack(msg_r.reshape(NC * 24, 128), 12)
    pl.semaphore_wait(line_y, 3)
    for peer in x_line:
        pl.semaphore_signal(line_x, inc=1, device_id=peer, device_id_type=MESH)

    def send_r(dx, k, dy):
        dz = 4 + ((k + 1) // 2) * (1 - 2 * (k % 2))
        ss, xx = ((z + dz) % NZ) * NY + (y + dy) % NY, (q + dx) % NX
        pltpu.make_async_remote_copy(
            msg_r.at[ss * NX + xx], r_own.at[:, q, s], send_sem, r_sem.at[dx],
            device_id=(ss * 2 + core, xx), device_id_type=MESH,
        ).start()
        return 0

    pltpu.make_async_copy(msg_r.at[chip], r_own.at[:, q, s], r_sem.at[0]).start()
    lax.fori_loop(0, 7, lambda o, _: send_r(0, o, 0), 0)
    lax.fori_loop(0, 24, lambda o, _: send_r(0, o // 3, 1 + o % 3), 0)
    pl.semaphore_wait(line_x, 3)
    lax.fori_loop(32, NC, lambda o, _: send_r(o // 32, (o // 4) % 8, o % 4), 0)

    lax.fori_loop(0, 6, left_rows, 0, unroll=UNROLL_PREP)
    pack(msg_l.reshape(NC * 12, 128), 6)

    def offset(g, e):
        return 4 - g if e == 0 else 4 + g + 4 * ((3 - g) // 3)

    def target(o):
        g, e = o // 32, o % 2
        dz = (4 - g) + e * (2 * g + 4 * ((3 - g) // 3))
        return ((z + dz) % NZ) * NY + (y + (o // 8)) % NY, (q + o // 2) % NX

    me = 1

    def to_all(send):
        send(0)
        lax.fori_loop(me + 1, NC, lambda o, _: send(o), 0)

    def send_l(o):
        ss, xx = target(o)
        pltpu.make_async_remote_copy(
            msg_l.at[ss * NX + xx], l_own.at[q, s], send_sem, l_sem.at[o // 32],
            device_id=(ss * 2 + core, xx), device_id_type=MESH,
        ).start()
        return 0

    pltpu.make_async_copy(msg_l.at[chip], l_own.at[q, s], l_sem.at[0]).start()
    to_all(send_l)

    def gates(i, _):
        gate[i] = jax.nn.sigmoid(jnp.dot(normed[i], w_in[4], preferred_element_type=F32))
        return 0

    lax.fori_loop(0, ROWS, gates, 0)

    def swap(dx, _):
        block = r_own.at[:, (q + NX - dx) % NX]
        mine = r_all.at[:, (q + NX - dx) % NX, :, core]
        pltpu.make_async_copy(block, block, r_sem.at[dx]).wait()
        pltpu.make_async_remote_copy(
            block, mine, swap_send, swap_sem, device_id=other, device_id_type=MESH
        ).start()
        pltpu.make_async_copy(block, mine, keep_sem).start()
        return 0

    lax.fori_loop(0, NX, swap, 0)
    pltpu.make_async_copy(r_own, r_own, keep_sem).wait()
    pltpu.make_async_copy(r_own, r_own, swap_sem).wait()

    ra = r_all.reshape(2 * NX * 768, 128)
    rb = r_own.reshape(2 * NX * 384, 128)
    la = l_own.reshape(NX * 384, 128)
    whole = t_a.reshape(NX * 384, 128)
    halves = t_b.reshape(NX * 192, 128)

    def block(ref, n, size):
        return ref[n * size : (n + 1) * size, :]

    for n, x in enumerate((0, 2)):
        r_mix[n] = jnp.concatenate(
            [block(ra, NX + x, 768)[:, 64:], block(ra, NX + x + 1, 768)[:, :64]], axis=1
        )
    lane_b = lax.broadcasted_iota(jnp.int32, (48, 128), 1) < 64

    def rows_of(g, _):
        places = [(z + NZ - offset(g, e)) % NZ for e in range(2)]
        arrived = msg_l.at[pl.ds(0, 32)]
        pltpu.make_async_copy(arrived, arrived, l_sem.at[g]).wait()

        def part(ref, n):
            return jnp.concatenate(
                [ref[pl.ds(pl.multiple_of(n * 384 + zz * 48, 48), 48), :] for zz in places], axis=0
            )

        lhs = [part(la, x) for x in range(NX)]
        for x in (0, 2):
            lhs.append(
                jnp.concatenate([part(rb, NX + x)[:, :64], part(rb, NX + x + 1)[:, 64:]], axis=1)
            )
        rhs = [block(ra, x, 768) for x in range(NX)] + [r_mix[0], r_mix[1]]
        triangle = lax.dot_general(
            jnp.concatenate(lhs, axis=1), jnp.concatenate(rhs, axis=1), (((1,), (1,)), ((), ())),
            preferred_element_type=F32,
        )
        for e, zz in enumerate(places):
            for x, tile in enumerate((0, 2, 3, 5)):
                whole[pl.ds(pl.multiple_of(x * 384 + zz * 48, 48), 48), :] = triangle[
                    e * 48 : (e + 1) * 48, tile * 128 : (tile + 1) * 128
                ].astype(BF16)

        def back(j, _):
            @pl.when((g != 0) | (j != me))
            def _():
                ss, xx = target(g * 32 + j)
                pltpu.make_async_remote_copy(
                    t_a.at[xx, ss], in_a.at[chip], send_sem, a_sem,
                    device_id=(ss * 2 + core, xx), device_id_type=MESH,
                ).start()

            return 0

        lax.fori_loop(0, 32, back, 0)
        for n, tile in enumerate((1, 4)):
            t_odd[n] = triangle[:, tile * 128 : (tile + 1) * 128]
            even, odd = t_odd[n, pl.ds(0, 48, stride=2), :], t_odd[n, pl.ds(1, 48, stride=2), :]
            both = (
                jnp.where(lane_b, even, pltpu.roll(odd, 64, 1)),
                jnp.where(lane_b, pltpu.roll(even, 64, 1), odd),
            )
            for e, zz in enumerate(places):
                for h in range(2):
                    halves[pl.ds(pl.multiple_of((2 * n + h) * 192 + zz * 24, 8), 24), :] = both[h][
                        e * 24 : (e + 1) * 24
                    ].astype(BF16)
        return 0

    lax.fori_loop(0, 4, rows_of, 0)
    pltpu.make_async_copy(t_a.at[q, s], in_a.at[chip], a_sem).start()
    pltpu.make_async_copy(t_b.at[q, s], in_b.at[chip], b_sem).start()

    def send_b(o):
        ss, xx = target(o)
        pltpu.make_async_remote_copy(
            t_b.at[xx, ss], in_b.at[chip], send_sem, b_sem,
            device_id=(ss * 2 + core, xx), device_id_type=MESH,
        ).start()
        return 0

    to_all(send_b)

    def unpack(source, steps):
        def some(n, _):
            rows = pl.ds(pl.multiple_of(n * 256, 256), 256)
            stage[rows, :] = source[rows, :].astype(F32)
            return 0

        lax.fori_loop(0, steps, some, 0)

    def projected(g, stride):
        scaled = unit_norm(stage[pl.ds(g, NC, stride=stride), :], 0)
        return jnp.dot(scaled.T.astype(BF16), w_in[5], preferred_element_type=F32)

    a0 = pl.multiple_of((q % 2) * 64, 64)
    b0 = pl.multiple_of((1 - q % 2) * 128, 128)

    def whole_rows(i, _):
        out_ref[i, pl.ds(a0, 128), :] = (gate[i, pl.ds(a0, 128), :] * projected(i, 12)).astype(BF16)
        return 0

    def half_rows(p, _):
        both = projected(p, 6)
        for e in range(2):
            out_ref[2 * p + e, pl.ds(b0, 64), :] = (
                gate[2 * p + e, pl.ds(b0, 64), :] * both[e * 64 : (e + 1) * 64]
            ).astype(BF16)
        return 0

    pltpu.make_async_copy(in_a, in_a, a_sem).wait()
    unpack(in_a.reshape(NC * 12, 128), 6)
    lax.fori_loop(0, 12, whole_rows, 0, unroll=UNROLL)
    pltpu.make_async_copy(in_b, in_b, b_sem).wait()
    unpack(in_b.reshape(NC * 6, 128), 3)
    lax.fori_loop(0, 6, half_rows, 0, unroll=UNROLL)
    for sent in (msg_r, msg_l, in_a, in_b):
        sent = sent.at[pl.ds(0, NC - 1)]
        pltpu.make_async_copy(sent, sent, send_sem).wait()
    pltpu.make_async_copy(r_own, r_own, swap_send).wait()


def local(*args):
    hbm = pl.BlockSpec(memory_space=pltpu.HBM)
    vmem = pl.BlockSpec(memory_space=pltpu.VMEM)
    dma = pltpu.SemaphoreType.DMA
    return pl.pallas_call(
        kernel,
        out_shape=jax.ShapeDtypeStruct((ROWS, COLS, WIDTH), BF16),
        in_specs=[hbm] * 8,
        out_specs=vmem,
        scratch_shapes=[
            pltpu.VMEM((ROWS, COLS, WIDTH), BF16),
            pltpu.SMEM((12, 12), jnp.int32),
            pltpu.VMEM((6, WIDTH, WIDTH), BF16),
            pltpu.VMEM((4 * WIDTH, WIDTH), BF16),
            pltpu.VMEM((ROWS, COLS, WIDTH), BF16),
            pltpu.VMEM((6, 256, WIDTH), BF16),
            pltpu.VMEM((ROWS, COLS, WIDTH), F32),
            pltpu.VMEM((NC * 24, 128), F32),
            pltpu.VMEM((NC, 2, 3, 4, 128), BF16),
            pltpu.VMEM((NC, 3, 4, 128), BF16),
            pltpu.VMEM((2, NX, NS, 3, 4, 128), BF16),
            pltpu.VMEM((2, NX, NS, 2, 3, 4, 128), BF16),
            pltpu.VMEM((2, 768, 128), BF16),
            pltpu.VMEM((NX, NS, 3, 4, 128), BF16),
            pltpu.VMEM((2, 96, 128), F32),
            pltpu.VMEM((NX, NS, 6, 2, 128), BF16),
            pltpu.VMEM((NX, NS, 3, 2, 128), BF16),
            pltpu.VMEM((NC, 6, 2, 128), BF16),
            pltpu.VMEM((NC, 3, 2, 128), BF16),
            dma((4,)), dma, dma((NX,)), dma((4,)), dma, dma, dma, dma, dma,
            pltpu.SemaphoreType.REGULAR, pltpu.SemaphoreType.REGULAR,
        ],
        compiler_params=pltpu.CompilerParams(
            collective_id=0, has_side_effects=True, vmem_limit_bytes=40 * 2**20
        ),
    )(*(pltpu.with_memory_space_constraint(a, pltpu.HBM) for a in args))


def solution(mesh):
    return jax.shard_map(
        local,
        mesh=mesh,
        in_specs=(P("row", "col", None), P(), P(), P(), P(), P(), P(), P()),
        out_specs=P("row", "col", None),
        check_vma=False,
    )
```

time: 63.3 us -> 57.6 us (0.910)
  Pallas kernels: 61.2 us -> 56.7 us
  local copies, waits for them, and re-layouts: 1.92 us -> 0.82 us
    pallas_call x1, Pallas kernels: 61.2 us -> 56.7 us  [local(): pl.pallas_call(kernel, out_shape=jax.ShapeDtypeStruct((ROWS, COLS, WIDTH)...]
    unnamed x1, local copies, waits for them, and re-layouts: 1.92 us -> 0.82 us
where the time goes in v3:
time: 57.6 us; the launch traced here: 57.5 us
  Pallas kernels  56.7 us (98%)
  local copies, waits for them, and re-layouts  0.82 us (1%)
    pallas_call x1, Pallas kernels, local(): pl.pallas_call(kernel, out_shape=jax.ShapeDtypeStruct((ROWS, COLS, WIDTH)...  56.7 us

profile of v3, /device:TPU:1, one launch (start us, length us, event | category | flops | bytes accessed | tf_op | source)
XLA Modules:
  0.0 57.5 jit_solution(7136714982081668731)
XLA Ops:
  0.0 56.7 %shard_map.82 = bf16[12,192,128]{2,1,0:T(8,128)(2,1)S(1)} custom-call(bf16[12,192,128]{2,1,0:T(8,128)(2,1)} %x_hbm.1, s32[12,12]{1,0:T(8,128)} %tm_hbm.1, bf16[128,128]{1,0:T(8,128)(2,1)} %wlg_hbm.1, bf16[128,128]{1,0:T(8,128)(2,1)} %wl_hbm.1, bf16[128,128]{1,0:T(8,128)(2,1)} %wrg_hbm.1, bf16[128,128]{1,0:T(8,128)(2,1)} %wr_hbm.1, bf16[128,128]{1,0:T(8,128)(2,1)} %wog_hbm.1, ...), custom_call_target="tpu_custom_call" | custom-call | tf_op jit(solution)/shard_map/pallas_call | solution.py:311
  56.7 0.8 %copy.10 = bf16[12,192,128]{2,1,0:T(8,128)(2,1)} copy(bf16[12,192,128]{2,1,0:T(8,128)(2,1)S(1)} %shard_map.82) | data formatting | bytes 1179648

commit v4 on v3

--- a/solution.py
+++ b/solution.py
@@ -23,7 +23,7 @@
 
 def kernel(
     x_hbm, tm_hbm, wlg_hbm, wl_hbm, wrg_hbm, wr_hbm, wog_hbm, wo_hbm, out_ref,
-    x_ref, tm_ref, w_in, wt, normed, masked, gate, stage, msg_r, msg_l, r_own, r_all, r_mix, l_own,
+    x_ref, tm_ref, w_in, wt, normed, masked, gate, stage, msg_r, msg_b, msg_l, r_own, r_all, r_mix, l_own,
     t_odd, t_a, t_b, in_a, in_b,
     load_sem, send_sem, r_sem, l_sem, a_sem, b_sem, swap_sem, swap_send, keep_sem, line_y, line_x,
 ):
@@ -45,6 +45,9 @@
     for load in load_x:
         load.start()
 
+    xs = [(q + d) % NX for d in range(NX)]
+    ys = [(y + d) % NY for d in range(NY)]
+
     def at(zz, yy, xx):
         return ((zz * NY + yy) * 2 + core, xx)
 
@@ -67,6 +70,9 @@
             wt[n * WIDTH : (n + 1) * WIDTH, :], values, (((1,), (1,)), ((), ())),
             preferred_element_type=F32,
         )
+
+    def store(n, rows):
+        stage[pl.ds(n, NC, stride=12), :] = rows
 
     def right_rows(p, _):
         parts = {}
@@ -79,87 +85,99 @@
                 m = tm_ref[tile, q * 3 + t].astype(F32)
                 parts[e, t] = (n[t * 64 : (t + 1) * 64] * m).astype(BF16)
         firsts = jnp.concatenate([parts[0, 0], parts[0, 1], parts[1, 0], parts[1, 1]], axis=0)
-        lasts = jnp.concatenate([parts[0, 2], parts[1, 2]], axis=0)
-        masked[p] = firsts
+        masked[p, 0:256, :] = firsts
+        masked[p, 256:384, :] = jnp.concatenate([parts[0, 2], parts[1, 2]], axis=0)
         right = jax.nn.sigmoid(project(2, firsts)) * project(3, firsts)
-        right_last = jax.nn.sigmoid(project(2, lasts)) * project(3, lasts)
-        left_last = jax.nn.sigmoid(project(0, lasts)) * project(1, lasts)
-        first = jnp.where(odd_q, right_last, left_last)
-        second = jnp.where(odd_q, left_last, right_last)
-        mixed = (
-            jnp.where(low, first, pltpu.roll(second, 64, 1)),
-            jnp.where(low, pltpu.roll(first, 64, 1), second),
-        )
         for e in range(2):
-            stage[pl.ds(2 * p + e, NC, stride=24), :] = right[:, e * 128 : (e + 1) * 128]
-            stage[pl.ds(12 + 2 * p + e, NC, stride=24), :] = mixed[e]
+            store(2 * p + e, right[:, e * 128 : (e + 1) * 128])
+        return 0
+
+    def shared_rows(p, _):
+        lasts = masked[p, 256:384, :]
+        right = jax.nn.sigmoid(project(2, lasts)) * project(3, lasts)
+        left = jax.nn.sigmoid(project(0, lasts)) * project(1, lasts)
+        first, second = jnp.where(odd_q, right, left), jnp.where(odd_q, left, right)
+        store(2 * p, jnp.where(low, first, pltpu.roll(second, 64, 1)))
+        store(2 * p + 1, jnp.where(low, pltpu.roll(first, 64, 1), second))
         return 0
 
     def left_rows(p, _):
-        left = jax.nn.sigmoid(project(0, masked[p])) * project(1, masked[p])
+        firsts = masked[p, 0:256, :]
+        left = jax.nn.sigmoid(project(0, firsts)) * project(1, firsts)
         for e in range(2):
-            stage[pl.ds(2 * p + e, NC, stride=12), :] = left[:, e * 128 : (e + 1) * 128]
-        return 0
-
-    def pack(target, steps):
+            store(2 * p + e, left[:, e * 128 : (e + 1) * 128])
+        return 0
+
+    def pack(message):
+        target = message.reshape(NC * 12, 128)
+
         def some(n, _):
             rows = pl.ds(pl.multiple_of(n * 256, 256), 256)
             target[rows, :] = stage[rows, :].astype(BF16)
             return 0
 
-        lax.fori_loop(0, steps, some, 0)
+        lax.fori_loop(0, 6, some, 0)
+
+    def send_r(kind, dx, k, dys):
+        zz, xx = (z + 4 + ((k + 1) // 2) * (1 - 2 * (k % 2))) % NZ, (q + dx) % NX
+        for dy in dys:
+            ss = zz * NY + ys[dy]
+            pltpu.make_async_remote_copy(
+                (msg_r, msg_b)[kind].at[ss * NX + xx], r_own.at[kind, q, s],
+                send_sem, r_sem.at[4 * kind + dx],
+                device_id=(ss * 2 + core, xx), device_id_type=MESH,
+            ).start()
+        return 0
 
     load_x[0].wait()
     lax.fori_loop(0, 3, right_rows, 0, unroll=UNROLL_PREP)
+    load_x[1].wait()
+    lax.fori_loop(3, 6, right_rows, 0, unroll=UNROLL_PREP)
+    pack(msg_r)
     pl.semaphore_wait(barrier, 1 + 3 + 3 + 7)
     for peer in y_line:
         pl.semaphore_signal(line_y, inc=1, device_id=peer, device_id_type=MESH)
-    load_x[1].wait()
-    lax.fori_loop(3, 6, right_rows, 0, unroll=UNROLL_PREP)
-    pack(msg_r.reshape(NC * 24, 128), 12)
+    pltpu.make_async_copy(msg_r.at[chip], r_own.at[0, q, s], r_sem.at[0]).start()
+    lax.fori_loop(0, 7, lambda k, _: send_r(0, 0, k, (0,)), 0)
     pl.semaphore_wait(line_y, 3)
     for peer in x_line:
         pl.semaphore_signal(line_x, inc=1, device_id=peer, device_id_type=MESH)
-
-    def send_r(dx, k, dy):
-        dz = 4 + ((k + 1) // 2) * (1 - 2 * (k % 2))
-        ss, xx = ((z + dz) % NZ) * NY + (y + dy) % NY, (q + dx) % NX
+    lax.fori_loop(0, 8, lambda k, _: send_r(0, 0, k, (1, 2, 3)), 0)
+    pl.semaphore_wait(line_x, 3)
+    lax.fori_loop(8, 32, lambda n, _: send_r(0, n // 8, n % 8, range(4)), 0)
+
+    lax.fori_loop(0, 6, shared_rows, 0, unroll=UNROLL_PREP)
+    pack(msg_b)
+    pltpu.make_async_copy(msg_b.at[chip], r_own.at[1, q, s], r_sem.at[4]).start()
+    lax.fori_loop(0, 7, lambda k, _: send_r(1, 0, k, range(4)), 0)
+    send_r(1, 0, 7, (1, 2, 3))
+    lax.fori_loop(8, 32, lambda n, _: send_r(1, n // 8, n % 8, range(4)), 0)
+
+    lax.fori_loop(0, 6, left_rows, 0, unroll=UNROLL_PREP)
+    pack(msg_l)
+
+    def offset(g, e):
+        return 4 - g if e == 0 else 4 + g + 4 * ((3 - g) // 3)
+
+    def to_all(send):
+        def eight(n, skip):
+            g = n // 4
+            yy = (y + n) % NY
+            for e in range(2):
+                ss = ((z + offset(g, e)) % NZ) * NY + yy
+                for d in range(NX):
+                    if (e, d) != skip:
+                        send(g, ss, xs[d])
+            return 0
+
+        eight(0, (1, 0))
+        lax.fori_loop(1, 16, lambda n, _: eight(n, None), 0)
+
+    def send_l(g, ss, xx):
         pltpu.make_async_remote_copy(
-            msg_r.at[ss * NX + xx], r_own.at[:, q, s], send_sem, r_sem.at[dx],
+            msg_l.at[ss * NX + xx], l_own.at[q, s], send_sem, l_sem.at[g],
             device_id=(ss * 2 + core, xx), device_id_type=MESH,
         ).start()
-        return 0
-
-    pltpu.make_async_copy(msg_r.at[chip], r_own.at[:, q, s], r_sem.at[0]).start()
-    lax.fori_loop(0, 7, lambda o, _: send_r(0, o, 0), 0)
-    lax.fori_loop(0, 24, lambda o, _: send_r(0, o // 3, 1 + o % 3), 0)
-    pl.semaphore_wait(line_x, 3)
-    lax.fori_loop(32, NC, lambda o, _: send_r(o // 32, (o // 4) % 8, o % 4), 0)
-
-    lax.fori_loop(0, 6, left_rows, 0, unroll=UNROLL_PREP)
-    pack(msg_l.reshape(NC * 12, 128), 6)
-
-    def offset(g, e):
-        return 4 - g if e == 0 else 4 + g + 4 * ((3 - g) // 3)
-
-    def target(o):
-        g, e = o // 32, o % 2
-        dz = (4 - g) + e * (2 * g + 4 * ((3 - g) // 3))
-        return ((z + dz) % NZ) * NY + (y + (o // 8)) % NY, (q + o // 2) % NX
-
-    me = 1
-
-    def to_all(send):
-        send(0)
-        lax.fori_loop(me + 1, NC, lambda o, _: send(o), 0)
-
-    def send_l(o):
-        ss, xx = target(o)
-        pltpu.make_async_remote_copy(
-            msg_l.at[ss * NX + xx], l_own.at[q, s], send_sem, l_sem.at[o // 32],
-            device_id=(ss * 2 + core, xx), device_id_type=MESH,
-        ).start()
-        return 0
 
     pltpu.make_async_copy(msg_l.at[chip], l_own.at[q, s], l_sem.at[0]).start()
     to_all(send_l)
@@ -170,17 +188,17 @@
 
     lax.fori_loop(0, ROWS, gates, 0)
 
-    def swap(dx, _):
-        block = r_own.at[:, (q + NX - dx) % NX]
-        mine = r_all.at[:, (q + NX - dx) % NX, :, core]
-        pltpu.make_async_copy(block, block, r_sem.at[dx]).wait()
+    def swap(n, _):
+        kind, xx = n // NX, (q + NX - n % NX) % NX
+        block, mine = r_own.at[kind, xx], r_all.at[kind, xx, :, core]
+        pltpu.make_async_copy(block, block, r_sem.at[n]).wait()
         pltpu.make_async_remote_copy(
             block, mine, swap_send, swap_sem, device_id=other, device_id_type=MESH
         ).start()
         pltpu.make_async_copy(block, mine, keep_sem).start()
         return 0
 
-    lax.fori_loop(0, NX, swap, 0)
+    lax.fori_loop(0, 2 * NX, swap, 0)
     pltpu.make_async_copy(r_own, r_own, keep_sem).wait()
     pltpu.make_async_copy(r_own, r_own, swap_sem).wait()
 
@@ -225,18 +243,24 @@
                     e * 48 : (e + 1) * 48, tile * 128 : (tile + 1) * 128
                 ].astype(BF16)
 
-        def back(j, _):
-            @pl.when((g != 0) | (j != me))
-            def _():
-                ss, xx = target(g * 32 + j)
-                pltpu.make_async_remote_copy(
-                    t_a.at[xx, ss], in_a.at[chip], send_sem, a_sem,
-                    device_id=(ss * 2 + core, xx), device_id_type=MESH,
-                ).start()
-
+        def back(dy, _):
+            for e, zz in enumerate(places):
+                ss = zz * NY + (y + dy) % NY
+                for d in range(NX):
+
+                    def send(ss=ss, xx=xs[d]):
+                        pltpu.make_async_remote_copy(
+                            t_a.at[xx, ss], in_a.at[chip], send_sem, a_sem,
+                            device_id=(ss * 2 + core, xx), device_id_type=MESH,
+                        ).start()
+
+                    if (e, d) == (1, 0):
+                        pl.when((g != 0) | (dy != 0))(send)
+                    else:
+                        send()
             return 0
 
-        lax.fori_loop(0, 32, back, 0)
+        lax.fori_loop(0, NY, back, 0)
         for n, tile in enumerate((1, 4)):
             t_odd[n] = triangle[:, tile * 128 : (tile + 1) * 128]
             even, odd = t_odd[n, pl.ds(0, 48, stride=2), :], t_odd[n, pl.ds(1, 48, stride=2), :]
@@ -255,13 +279,11 @@
     pltpu.make_async_copy(t_a.at[q, s], in_a.at[chip], a_sem).start()
     pltpu.make_async_copy(t_b.at[q, s], in_b.at[chip], b_sem).start()
 
-    def send_b(o):
-        ss, xx = target(o)
+    def send_b(g, ss, xx):
         pltpu.make_async_remote_copy(
             t_b.at[xx, ss], in_b.at[chip], send_sem, b_sem,
             device_id=(ss * 2 + core, xx), device_id_type=MESH,
         ).start()
-        return 0
 
     to_all(send_b)
 
@@ -298,7 +320,7 @@
     pltpu.make_async_copy(in_b, in_b, b_sem).wait()
     unpack(in_b.reshape(NC * 6, 128), 3)
     lax.fori_loop(0, 6, half_rows, 0, unroll=UNROLL)
-    for sent in (msg_r, msg_l, in_a, in_b):
+    for sent in (msg_r, msg_b, msg_l, in_a, in_b):
         sent = sent.at[pl.ds(0, NC - 1)]
         pltpu.make_async_copy(sent, sent, send_sem).wait()
     pltpu.make_async_copy(r_own, r_own, swap_send).wait()
@@ -319,10 +341,11 @@
             pltpu.VMEM((6, WIDTH, WIDTH), BF16),
             pltpu.VMEM((4 * WIDTH, WIDTH), BF16),
             pltpu.VMEM((ROWS, COLS, WIDTH), BF16),
-            pltpu.VMEM((6, 256, WIDTH), BF16),
+            pltpu.VMEM((6, 384, WIDTH), BF16),
             pltpu.VMEM((ROWS, COLS, WIDTH), F32),
-            pltpu.VMEM((NC * 24, 128), F32),
-            pltpu.VMEM((NC, 2, 3, 4, 128), BF16),
+            pltpu.VMEM((NC * 12, 128), F32),
+            pltpu.VMEM((NC, 3, 4, 128), BF16),
+            pltpu.VMEM((NC, 3, 4, 128), BF16),
             pltpu.VMEM((NC, 3, 4, 128), BF16),
             pltpu.VMEM((2, NX, NS, 3, 4, 128), BF16),
             pltpu.VMEM((2, NX, NS, 2, 3, 4, 128), BF16),
@@ -333,7 +356,7 @@
             pltpu.VMEM((NX, NS, 3, 2, 128), BF16),
             pltpu.VMEM((NC, 6, 2, 128), BF16),
             pltpu.VMEM((NC, 3, 2, 128), BF16),
-            dma((4,)), dma, dma((NX,)), dma((4,)), dma, dma, dma, dma, dma,
+            dma((4,)), dma, dma((2 * NX,)), dma((4,)), dma, dma, dma, dma, dma,
             pltpu.SemaphoreType.REGULAR, pltpu.SemaphoreType.REGULAR,
         ],
         compiler_params=pltpu.CompilerParams(

time: 57.6 us -> 56.3 us (0.977)
  Pallas kernels: 56.7 us -> 55.4 us
    pallas_call x1, Pallas kernels: 56.7 us -> 55.4 us  [local(): pl.pallas_call(kernel, out_shape=jax.ShapeDtypeStruct((ROWS, COLS, WIDTH)...]
where the time goes in v4:
time: 56.3 us; the launch traced here: 56.2 us
  Pallas kernels  55.4 us (98%)
  local copies, waits for them, and re-layouts  0.82 us (1%)
    pallas_call x1, Pallas kernels, local(): pl.pallas_call(kernel, out_shape=jax.ShapeDtypeStruct((ROWS, COLS, WIDTH)...  55.4 us

profile of v4, /device:TPU:1, one launch (start us, length us, event | category | flops | bytes accessed | tf_op | source)
XLA Modules:
  0.0 56.2 jit_solution(15749208723311980007)
XLA Ops:
  0.0 55.4 %shard_map.82 = bf16[12,192,128]{2,1,0:T(8,128)(2,1)S(1)} custom-call(bf16[12,192,128]{2,1,0:T(8,128)(2,1)} %x_hbm.1, s32[12,12]{1,0:T(8,128)} %tm_hbm.1, bf16[128,128]{1,0:T(8,128)(2,1)} %wlg_hbm.1, bf16[128,128]{1,0:T(8,128)(2,1)} %wl_hbm.1, bf16[128,128]{1,0:T(8,128)(2,1)} %wrg_hbm.1, bf16[128,128]{1,0:T(8,128)(2,1)} %wr_hbm.1, bf16[128,128]{1,0:T(8,128)(2,1)} %wog_hbm.1, ...), custom_call_target="tpu_custom_call" | custom-call | tf_op jit(solution)/shard_map/pallas_call | solution.py:333
  55.4 0.8 %copy.10 = bf16[12,192,128]{2,1,0:T(8,128)(2,1)} copy(bf16[12,192,128]{2,1,0:T(8,128)(2,1)S(1)} %shard_map.82) | data formatting | bytes 1179648

commit v5 on v4

--- a/solution.py
+++ b/solution.py
@@ -11,7 +11,7 @@
 NX, NY, NZ, NS, NC = 4, 4, 8, 32, 128
 ROWS, COLS, WIDTH = 12, 192, 128
 F32, BF16 = jnp.float32, jnp.bfloat16
-UNROLL, UNROLL_PREP = 3, 3
+UNROLL, UNROLL_PREP = 6, 3
 
 
 def unit_norm(values, axis):
@@ -297,7 +297,9 @@
 
     def projected(g, stride):
         scaled = unit_norm(stage[pl.ds(g, NC, stride=stride), :], 0)
-        return jnp.dot(scaled.T.astype(BF16), w_in[5], preferred_element_type=F32)
+        return lax.dot_general(
+            scaled.astype(BF16), w_in[5], (((0,), (0,)), ((), ())), preferred_element_type=F32
+        )
 
     a0 = pl.multiple_of((q % 2) * 64, 64)
     b0 = pl.multiple_of((1 - q % 2) * 128, 128)

time: 56.3 us -> 56 us (level)
  no operation moved by 1% of the time
where the time goes in v5:
time: 56 us; the launch traced here: 55.9 us
  Pallas kernels  55.1 us (98%)
  local copies, waits for them, and re-layouts  0.82 us (1%)
    pallas_call x1, Pallas kernels, local(): pl.pallas_call(kernel, out_shape=jax.ShapeDtypeStruct((ROWS, COLS, WIDTH)...  55.1 us

profile of v5, /device:TPU:1, one launch (start us, length us, event | category | flops | bytes accessed | tf_op | source)
XLA Modules:
  0.0 55.9 jit_solution(2176054371650295983)
XLA Ops:
  0.0 55.1 %shard_map.82 = bf16[12,192,128]{2,1,0:T(8,128)(2,1)S(1)} custom-call(bf16[12,192,128]{2,1,0:T(8,128)(2,1)} %x_hbm.1, s32[12,12]{1,0:T(8,128)} %tm_hbm.1, bf16[128,128]{1,0:T(8,128)(2,1)} %wlg_hbm.1, bf16[128,128]{1,0:T(8,128)(2,1)} %wl_hbm.1, bf16[128,128]{1,0:T(8,128)(2,1)} %wrg_hbm.1, bf16[128,128]{1,0:T(8,128)(2,1)} %wr_hbm.1, bf16[128,128]{1,0:T(8,128)(2,1)} %wog_hbm.1, ...), custom_call_target="tpu_custom_call" | custom-call | tf_op jit(solution)/shard_map/pallas_call | solution.py:335
  55.1 0.8 %copy.10 = bf16[12,192,128]{2,1,0:T(8,128)(2,1)} copy(bf16[12,192,128]{2,1,0:T(8,128)(2,1)S(1)} %shard_map.82) | data formatting | bytes 1179648

commit v6 on v5

--- a/solution.py
+++ b/solution.py
@@ -23,14 +23,15 @@
 
 def kernel(
     x_hbm, tm_hbm, wlg_hbm, wl_hbm, wrg_hbm, wr_hbm, wog_hbm, wo_hbm, out_ref,
-    x_ref, tm_ref, w_in, wt, normed, masked, gate, stage, msg_r, msg_b, msg_l, r_own, r_all, r_mix, l_own,
+    x_ref, tm_ref, w_in, wt, normed, masked, gate, stage, msg_r, msg_b, msg_l, r_own, r_all, r_half, r_mix, l_own,
     t_odd, t_a, t_b, in_a, in_b,
-    load_sem, send_sem, r_sem, l_sem, a_sem, b_sem, swap_sem, swap_send, keep_sem, line_y, line_x,
+    load_sem, send_sem, r_sem, l_sem, a_sem, b_sem, relay_sem, relay_send, swap_sem, swap_send, keep_sem,
+    line_y, line_x,
 ):
     row, q = lax.axis_index("row"), lax.axis_index("col")
     core, y, z = row % 2, (row // 2) % NY, row // (2 * NY)
     s = row // 2
-    chip = s * NX + q
+    channels = [s * NX + q, (((z + NZ - 1) % NZ) * NY + y) * NX + q]
     other = ((s * 2) + 1 - core, q)
 
     weights = (wlg_hbm, wl_hbm, wrg_hbm, wr_hbm, wog_hbm, wo_hbm)
@@ -118,16 +119,27 @@
 
         lax.fori_loop(0, 6, some, 0)
 
-    def send_r(kind, dx, k, dys):
-        zz, xx = (z + 4 + ((k + 1) // 2) * (1 - 2 * (k % 2))) % NZ, (q + dx) % NX
+    def ends(k):
+        slot = k % 2
+        zz = (z + NZ + (3 - k // 2) * (1 - 2 * slot)) % NZ
+        return slot, zz, (zz + NZ - slot) % NZ
+
+    def send_r(kind, k, dxs, dys):
+        slot, zz, d = ends(k)
         for dy in dys:
-            ss = zz * NY + ys[dy]
-            pltpu.make_async_remote_copy(
-                (msg_r, msg_b)[kind].at[ss * NX + xx], r_own.at[kind, q, s],
-                send_sem, r_sem.at[4 * kind + dx],
-                device_id=(ss * 2 + core, xx), device_id_type=MESH,
+            for dx in dxs:
+                pltpu.make_async_remote_copy(
+                    (msg_r, msg_b)[kind].at[(d * NY + ys[dy]) * NX + xs[dx]],
+                    r_own.at[kind, slot, q, s], send_sem, r_sem.at[4 * kind + k // 2],
+                    device_id=((zz * NY + ys[dy]) * 2 + core, xs[dx]), device_id_type=MESH,
+                ).start()
+        return 0
+
+    def keep_r(kind):
+        for slot in range(2):
+            pltpu.make_async_copy(
+                (msg_r, msg_b)[kind].at[channels[slot]], r_own.at[kind, slot, q, s], r_sem.at[4 * kind + 3]
             ).start()
-        return 0
 
     load_x[0].wait()
     lax.fori_loop(0, 3, right_rows, 0, unroll=UNROLL_PREP)
@@ -137,50 +149,114 @@
     pl.semaphore_wait(barrier, 1 + 3 + 3 + 7)
     for peer in y_line:
         pl.semaphore_signal(line_y, inc=1, device_id=peer, device_id_type=MESH)
-    pltpu.make_async_copy(msg_r.at[chip], r_own.at[0, q, s], r_sem.at[0]).start()
-    lax.fori_loop(0, 7, lambda k, _: send_r(0, 0, k, (0,)), 0)
+    keep_r(0)
+    lax.fori_loop(0, 6, lambda k, _: send_r(0, k, (0,), (0,)), 0)
     pl.semaphore_wait(line_y, 3)
     for peer in x_line:
         pl.semaphore_signal(line_x, inc=1, device_id=peer, device_id_type=MESH)
-    lax.fori_loop(0, 8, lambda k, _: send_r(0, 0, k, (1, 2, 3)), 0)
+    lax.fori_loop(0, 8, lambda k, _: send_r(0, k, (0,), (1, 2, 3)), 0)
     pl.semaphore_wait(line_x, 3)
-    lax.fori_loop(8, 32, lambda n, _: send_r(0, n // 8, n % 8, range(4)), 0)
+    lax.fori_loop(0, 8, lambda k, _: send_r(0, k, (1, 2, 3), range(4)), 0)
 
     lax.fori_loop(0, 6, shared_rows, 0, unroll=UNROLL_PREP)
     pack(msg_b)
-    pltpu.make_async_copy(msg_b.at[chip], r_own.at[1, q, s], r_sem.at[4]).start()
-    lax.fori_loop(0, 7, lambda k, _: send_r(1, 0, k, range(4)), 0)
-    send_r(1, 0, 7, (1, 2, 3))
-    lax.fori_loop(8, 32, lambda n, _: send_r(1, n // 8, n % 8, range(4)), 0)
+    keep_r(1)
+    lax.fori_loop(0, 6, lambda k, _: send_r(1, k, range(4), range(4)), 0)
+
+    def near(k, _):
+        send_r(1, k, range(1, 4), range(1))
+        return send_r(1, k, range(4), range(1, 4))
+
+    lax.fori_loop(6, 8, near, 0)
 
     lax.fori_loop(0, 6, left_rows, 0, unroll=UNROLL_PREP)
     pack(msg_l)
 
-    def offset(g, e):
-        return 4 - g if e == 0 else 4 + g + 4 * ((3 - g) // 3)
-
-    def to_all(send):
-        def eight(n, skip):
-            g = n // 4
-            yy = (y + n) % NY
-            for e in range(2):
-                ss = ((z + offset(g, e)) % NZ) * NY + yy
-                for d in range(NX):
-                    if (e, d) != skip:
-                        send(g, ss, xs[d])
-            return 0
-
-        eight(0, (1, 0))
-        lax.fori_loop(1, 16, lambda n, _: eight(n, None), 0)
-
-    def send_l(g, ss, xx):
+    def four(zz):
+        return pl.ds(((zz + NZ) % NZ) * NY, NY)
+
+    def send_l(k, dys, dxs):
+        slot, zz, d = ends(k)
+        for dy in dys:
+            for dx in dxs:
+                pltpu.make_async_remote_copy(
+                    msg_l.at[(d * NY + ys[dy]) * NX + xs[dx]], l_own.at[slot, q, s],
+                    send_sem, l_sem.at[((k + 6) // 8) * 2 + slot],
+                    device_id=((zz * NY + ys[dy]) * 2 + core, xs[dx]), device_id_type=MESH,
+                ).start()
+
+    rb = r_own.reshape(2 * 2 * NX * 384, 128)
+    rh = r_half.reshape(2 * 2 * 384, 128)
+
+    def to_partner(kind, source, target):
         pltpu.make_async_remote_copy(
-            msg_l.at[ss * NX + xx], l_own.at[q, s], send_sem, l_sem.at[g],
-            device_id=(ss * 2 + core, xx), device_id_type=MESH,
+            source, target, swap_send.at[kind], swap_sem.at[kind], device_id=other, device_id_type=MESH
         ).start()
 
-    pltpu.make_async_copy(msg_l.at[chip], l_own.at[q, s], l_sem.at[0]).start()
-    to_all(send_l)
+    def to_owner(kind, n, step, source, target):
+        pltpu.make_async_remote_copy(
+            source, target, relay_send.at[kind], relay_sem.at[n],
+            device_id=at((z + NZ + step) % NZ, y, q), device_id_type=MESH,
+        ).start()
+
+    def arrived(n):
+        block = r_own.at[0, 0, 0]
+        pltpu.make_async_copy(block, block, r_sem.at[n]).wait()
+
+    sides = ((0, 1), (1, -1))
+
+    def forward_right(n, _):
+        a = 3 - n
+        arrived(n)
+        moves = [(slot, step, xx, four(z - a * step)) for xx in range(NX) for slot, step in sides]
+        for slot, step, xx, place in moves:
+            to_owner(0, n, step, r_own.at[0, slot, xx, place], r_all.at[1 - slot, xx, place, core])
+        for slot, step, xx, place in moves:
+            block, mine = r_own.at[0, slot, xx, place], r_all.at[slot, xx, place, core]
+            to_partner(0, block, mine)
+            pltpu.make_async_copy(block, mine, keep_sem.at[0]).start()
+        return 0
+
+    def forward_shared(n, _):
+        a = 7 - n
+        arrived(n)
+        moves = []
+        for pair in range(2):
+            for slot, step in sides:
+                zz = (z + NZ - a * step) % NZ
+
+                def part(x):
+                    start = ((2 + slot) * NX + x) * 384 + zz * 48
+                    return rb[pl.ds(pl.multiple_of(start, 48), 48), :]
+
+                rh[pl.ds(pl.multiple_of((slot * 2 + pair) * 384 + zz * 48, 48), 48), :] = jnp.concatenate(
+                    [part(2 * pair)[:, 64:], part(2 * pair + 1)[:, :64]], axis=1
+                )
+                moves.append((slot, step, pair, pl.ds(zz * NY, NY)))
+        for slot, step, pair, place in moves:
+            to_owner(1, n, step, r_half.at[slot, pair, place], r_mix.at[1 - slot, pair, place, core])
+        for slot, step, pair, place in moves:
+            block, mine = r_half.at[slot, pair, place], r_mix.at[slot, pair, place, core]
+            to_partner(1, block, mine)
+            pltpu.make_async_copy(block, mine, keep_sem.at[1]).start()
+        return 0
+
+    for slot in range(2):
+        pltpu.make_async_copy(msg_l.at[channels[slot]], l_own.at[slot, q, s], l_sem.at[2 + slot]).start()
+    def left_to(k, _):
+        send_l(k, range(4), range(4))
+        return 0
+
+    def left_near(k, _):
+        send_l(k, range(1), range(1, 4))
+        send_l(k, range(1, 4), range(4))
+        return 0
+
+    lax.fori_loop(0, 4, forward_right, 0)
+    lax.fori_loop(4, 8, forward_shared, 0)
+    lax.fori_loop(0, 4, left_to, 0)
+    lax.fori_loop(4, 6, left_to, 0)
+    lax.fori_loop(6, 8, left_near, 0)
 
     def gates(i, _):
         gate[i] = jax.nn.sigmoid(jnp.dot(normed[i], w_in[4], preferred_element_type=F32))
@@ -188,58 +264,71 @@
 
     lax.fori_loop(0, ROWS, gates, 0)
 
-    def swap(n, _):
-        kind, xx = n // NX, (q + NX - n % NX) % NX
-        block, mine = r_own.at[kind, xx], r_all.at[kind, xx, :, core]
-        pltpu.make_async_copy(block, block, r_sem.at[n]).wait()
-        pltpu.make_async_remote_copy(
-            block, mine, swap_send, swap_sem, device_id=other, device_id_type=MESH
-        ).start()
-        pltpu.make_async_copy(block, mine, keep_sem).start()
-        return 0
-
-    lax.fori_loop(0, 2 * NX, swap, 0)
-    pltpu.make_async_copy(r_own, r_own, keep_sem).wait()
-    pltpu.make_async_copy(r_own, r_own, swap_sem).wait()
+    def relayed_right(n, _):
+        block = r_own.at[0, 0, 0]
+        pltpu.make_async_copy(block, block, relay_sem.at[n]).wait()
+        for xx in range(NX):
+            for slot, step in sides:
+                block = r_all.at[slot, xx, four(z + (4 - n) * step), core]
+                to_partner(0, block, block)
+        return 0
+
+    def relayed_shared(n, _):
+        block = r_own.at[0, 0, 0, pl.ds(0, 16)]
+        pltpu.make_async_copy(block, block, relay_sem.at[n]).wait()
+        for pair in range(2):
+            for slot, step in sides:
+                block = r_mix.at[slot, pair, four(z + (8 - n) * step), core]
+                to_partner(1, block, block)
+        return 0
+
+    lax.fori_loop(0, 4, relayed_right, 0)
+    lax.fori_loop(4, 8, relayed_shared, 0)
+    sizes = (r_own.at[0, 0], r_own.at[0, 0, pl.ds(0, 2)])
+    swaps = (r_own.at[0], r_own.at[0, 0])
+    for kind in range(2):
+        pltpu.make_async_copy(sizes[kind], sizes[kind], keep_sem.at[kind]).wait()
+        pltpu.make_async_copy(swaps[kind], swaps[kind], swap_sem.at[kind]).wait()
 
     ra = r_all.reshape(2 * NX * 768, 128)
-    rb = r_own.reshape(2 * NX * 384, 128)
-    la = l_own.reshape(NX * 384, 128)
-    whole = t_a.reshape(NX * 384, 128)
-    halves = t_b.reshape(NX * 192, 128)
+    rm = r_mix.reshape(2 * 2 * 768, 128)
+    la = l_own.reshape(2 * NX * 384, 128)
+    whole = t_a.reshape(2 * NX * 384, 128)
+    halves = t_b.reshape(2 * NX * 192, 128)
 
     def block(ref, n, size):
-        return ref[n * size : (n + 1) * size, :]
-
-    for n, x in enumerate((0, 2)):
-        r_mix[n] = jnp.concatenate(
-            [block(ra, NX + x, 768)[:, 64:], block(ra, NX + x + 1, 768)[:, :64]], axis=1
-        )
-    lane_b = lax.broadcasted_iota(jnp.int32, (48, 128), 1) < 64
-
-    def rows_of(g, _):
-        places = [(z + NZ - offset(g, e)) % NZ for e in range(2)]
-        arrived = msg_l.at[pl.ds(0, 32)]
-        pltpu.make_async_copy(arrived, arrived, l_sem.at[g]).wait()
+        return ref[pl.ds(pl.multiple_of(n * size, size), size), :]
+
+    lane_b = lax.broadcasted_iota(jnp.int32, (72, 128), 1) < 64
+
+    def rows_of(slot, which, distances):
+        count = len(distances)
+        places = [(z + NZ - a * (1 - 2 * slot)) % NZ for a in distances]
+        channel = channels[0] - slot * (channels[0] - channels[1])
+        arrived = msg_l.at[pl.ds(0, 16 * count)]
+        pltpu.make_async_copy(arrived, arrived, l_sem.at[which * 2 + slot]).wait()
 
         def part(ref, n):
             return jnp.concatenate(
                 [ref[pl.ds(pl.multiple_of(n * 384 + zz * 48, 48), 48), :] for zz in places], axis=0
             )
 
-        lhs = [part(la, x) for x in range(NX)]
+        lhs = [part(la, slot * NX + x) for x in range(NX)]
         for x in (0, 2):
+            first = (2 + slot) * NX + x
             lhs.append(
-                jnp.concatenate([part(rb, NX + x)[:, :64], part(rb, NX + x + 1)[:, 64:]], axis=1)
+                jnp.concatenate([part(rb, first)[:, :64], part(rb, first + 1)[:, 64:]], axis=1)
             )
-        rhs = [block(ra, x, 768) for x in range(NX)] + [r_mix[0], r_mix[1]]
+        rhs = [block(ra, slot * NX + x, 768) for x in range(NX)] + [
+            block(rm, slot * 2 + n, 768) for n in range(2)
+        ]
         triangle = lax.dot_general(
             jnp.concatenate(lhs, axis=1), jnp.concatenate(rhs, axis=1), (((1,), (1,)), ((), ())),
             preferred_element_type=F32,
         )
         for e, zz in enumerate(places):
             for x, tile in enumerate((0, 2, 3, 5)):
-                whole[pl.ds(pl.multiple_of(x * 384 + zz * 48, 48), 48), :] = triangle[
+                whole[pl.ds(pl.multiple_of((slot * NX + x) * 384 + zz * 48, 48), 48), :] = triangle[
                     e * 48 : (e + 1) * 48, tile * 128 : (tile + 1) * 128
                 ].astype(BF16)
 
@@ -250,42 +339,52 @@
 
                     def send(ss=ss, xx=xs[d]):
                         pltpu.make_async_remote_copy(
-                            t_a.at[xx, ss], in_a.at[chip], send_sem, a_sem,
+                            t_a.at[slot, xx, ss], in_a.at[channel], send_sem, a_sem,
                             device_id=(ss * 2 + core, xx), device_id_type=MESH,
                         ).start()
 
-                    if (e, d) == (1, 0):
-                        pl.when((g != 0) | (dy != 0))(send)
+                    if (distances[e], d) == (0, 0):
+                        pl.when(dy != 0)(send)
                     else:
                         send()
             return 0
 
         lax.fori_loop(0, NY, back, 0)
         for n, tile in enumerate((1, 4)):
-            t_odd[n] = triangle[:, tile * 128 : (tile + 1) * 128]
-            even, odd = t_odd[n, pl.ds(0, 48, stride=2), :], t_odd[n, pl.ds(1, 48, stride=2), :]
+            t_odd[n, 0 : count * 48, :] = triangle[:, tile * 128 : (tile + 1) * 128]
+            even, odd = (t_odd[n, pl.ds(h, count * 24, stride=2), :] for h in range(2))
+            lanes = lane_b[0 : count * 24]
             both = (
-                jnp.where(lane_b, even, pltpu.roll(odd, 64, 1)),
-                jnp.where(lane_b, pltpu.roll(even, 64, 1), odd),
+                jnp.where(lanes, even, pltpu.roll(odd, 64, 1)),
+                jnp.where(lanes, pltpu.roll(even, 64, 1), odd),
             )
             for e, zz in enumerate(places):
                 for h in range(2):
-                    halves[pl.ds(pl.multiple_of((2 * n + h) * 192 + zz * 24, 8), 24), :] = both[h][
+                    halves[pl.ds(pl.multiple_of((slot * NX + 2 * n + h) * 192 + zz * 24, 8), 24), :] = both[h][
                         e * 24 : (e + 1) * 24
                     ].astype(BF16)
         return 0
 
-    lax.fori_loop(0, 4, rows_of, 0)
-    pltpu.make_async_copy(t_a.at[q, s], in_a.at[chip], a_sem).start()
-    pltpu.make_async_copy(t_b.at[q, s], in_b.at[chip], b_sem).start()
-
-    def send_b(g, ss, xx):
-        pltpu.make_async_remote_copy(
-            t_b.at[xx, ss], in_b.at[chip], send_sem, b_sem,
-            device_id=(ss * 2 + core, xx), device_id_type=MESH,
-        ).start()
-
-    to_all(send_b)
+    def send_b(k, pairs):
+        slot = k % 2
+        zz = (z + NZ - (3 - k // 2) * (1 - 2 * slot)) % NZ
+        for dy, dx in pairs:
+            pltpu.make_async_remote_copy(
+                t_b.at[slot, xs[dx], (zz * NY) + ys[dy]],
+                in_b.at[channels[0] - slot * (channels[0] - channels[1])], send_sem, b_sem,
+                device_id=((zz * NY + ys[dy]) * 2 + core, xs[dx]), device_id_type=MESH,
+            ).start()
+        return 0
+
+    every = [(dy, dx) for dy in range(NY) for dx in range(NX)]
+    lax.fori_loop(0, 2, lambda slot, _: rows_of(slot, 0, (3,)), 0)
+    lax.fori_loop(0, 2, lambda k, _: send_b(k, every), 0)
+    lax.fori_loop(0, 2, lambda slot, _: rows_of(slot, 1, (2, 1, 0)), 0)
+    for slot in range(2):
+        pltpu.make_async_copy(t_a.at[slot, q, s], in_a.at[channels[slot]], a_sem).start()
+        pltpu.make_async_copy(t_b.at[slot, q, s], in_b.at[channels[slot]], b_sem).start()
+    lax.fori_loop(2, 6, lambda k, _: send_b(k, every), 0)
+    lax.fori_loop(6, 8, lambda k, _: send_b(k, every[1:]), 0)
 
     def unpack(source, steps):
         def some(n, _):
@@ -323,9 +422,11 @@
     unpack(in_b.reshape(NC * 6, 128), 3)
     lax.fori_loop(0, 6, half_rows, 0, unroll=UNROLL)
     for sent in (msg_r, msg_b, msg_l, in_a, in_b):
-        sent = sent.at[pl.ds(0, NC - 1)]
+        sent = sent.at[pl.ds(0, NC - 2)]
         pltpu.make_async_copy(sent, sent, send_sem).wait()
-    pltpu.make_async_copy(r_own, r_own, swap_send).wait()
+    for kind in range(2):
+        pltpu.make_async_copy(sizes[kind], sizes[kind], relay_send.at[kind]).wait()
+        pltpu.make_async_copy(swaps[kind], swaps[kind], swap_send.at[kind]).wait()
 
 
 def local(*args):
@@ -349,16 +450,18 @@
             pltpu.VMEM((NC, 3, 4, 128), BF16),
             pltpu.VMEM((NC, 3, 4, 128), BF16),
             pltpu.VMEM((NC, 3, 4, 128), BF16),
+            pltpu.VMEM((2, 2, NX, NS, 3, 4, 128), BF16),
+            pltpu.VMEM((2, NX, NS, 2, 3, 4, 128), BF16),
+            pltpu.VMEM((2, 2, NS, 3, 4, 128), BF16),
+            pltpu.VMEM((2, 2, NS, 2, 3, 4, 128), BF16),
             pltpu.VMEM((2, NX, NS, 3, 4, 128), BF16),
-            pltpu.VMEM((2, NX, NS, 2, 3, 4, 128), BF16),
-            pltpu.VMEM((2, 768, 128), BF16),
-            pltpu.VMEM((NX, NS, 3, 4, 128), BF16),
-            pltpu.VMEM((2, 96, 128), F32),
-            pltpu.VMEM((NX, NS, 6, 2, 128), BF16),
-            pltpu.VMEM((NX, NS, 3, 2, 128), BF16),
+            pltpu.VMEM((2, 144, 128), F32),
+            pltpu.VMEM((2, NX, NS, 6, 2, 128), BF16),
+            pltpu.VMEM((2, NX, NS, 3, 2, 128), BF16),
             pltpu.VMEM((NC, 6, 2, 128), BF16),
             pltpu.VMEM((NC, 3, 2, 128), BF16),
-            dma((4,)), dma, dma((2 * NX,)), dma((4,)), dma, dma, dma, dma, dma,
+            dma((4,)), dma, dma((2 * NX,)), dma((4,)), dma, dma,
+            dma((2 * NX,)), dma((2,)), dma((2,)), dma((2,)), dma((2,)),
             pltpu.SemaphoreType.REGULAR, pltpu.SemaphoreType.REGULAR,
         ],
         compiler_params=pltpu.CompilerParams(

time: 56 us -> 54.1 us (0.966)
  Pallas kernels: 55.1 us -> 52.7 us
    pallas_call x1, Pallas kernels: 55.1 us -> 52.7 us  [local(): pl.pallas_call(kernel, out_shape=jax.ShapeDtypeStruct((ROWS, COLS, WIDTH)...]
where the time goes in v6:
time: 54.1 us; the launch traced here: 53.6 us
  Pallas kernels  52.7 us (97%)
  local copies, waits for them, and re-layouts  0.82 us (2%)
    pallas_call x1, Pallas kernels, local(): pl.pallas_call(kernel, out_shape=jax.ShapeDtypeStruct((ROWS, COLS, WIDTH)...  52.7 us

profile of v6, /device:TPU:1, one launch (start us, length us, event | category | flops | bytes accessed | tf_op | source)
XLA Modules:
  0.0 53.6 jit_solution(1105353706166125788)
XLA Ops:
  0.0 52.7 %shard_map.82 = bf16[12,192,128]{2,1,0:T(8,128)(2,1)S(1)} custom-call(bf16[12,192,128]{2,1,0:T(8,128)(2,1)} %x_hbm.1, s32[12,12]{1,0:T(8,128)} %tm_hbm.1, bf16[128,128]{1,0:T(8,128)(2,1)} %wlg_hbm.1, bf16[128,128]{1,0:T(8,128)(2,1)} %wl_hbm.1, bf16[128,128]{1,0:T(8,128)(2,1)} %wrg_hbm.1, bf16[128,128]{1,0:T(8,128)(2,1)} %wr_hbm.1, bf16[128,128]{1,0:T(8,128)(2,1)} %wog_hbm.1, ...), custom_call_target="tpu_custom_call" | custom-call | tf_op jit(solution)/shard_map/pallas_call | solution.py:436
  52.7 0.8 %copy.10 = bf16[12,192,128]{2,1,0:T(8,128)(2,1)} copy(bf16[12,192,128]{2,1,0:T(8,128)(2,1)S(1)} %shard_map.82) | data formatting | bytes 1179648

commit v7 on v6

--- a/solution.py
+++ b/solution.py
@@ -205,8 +205,13 @@
 
     sides = ((0, 1), (1, -1))
 
+    def gates(i, _):
+        gate[i] = jax.nn.sigmoid(jnp.dot(normed[i], w_in[4], preferred_element_type=F32))
+        return 0
+
     def forward_right(n, _):
         a = 3 - n
+        lax.fori_loop(3 * n, 3 * n + 3, gates, 0)
         arrived(n)
         moves = [(slot, step, xx, four(z - a * step)) for xx in range(NX) for slot, step in sides]
         for slot, step, xx, place in moves:
@@ -215,6 +220,15 @@
             block, mine = r_own.at[0, slot, xx, place], r_all.at[slot, xx, place, core]
             to_partner(0, block, mine)
             pltpu.make_async_copy(block, mine, keep_sem.at[0]).start()
+        return 0
+
+    def relayed_right(n, _):
+        block = r_own.at[0, 0, 0]
+        pltpu.make_async_copy(block, block, relay_sem.at[n]).wait()
+        for xx in range(NX):
+            for slot, step in sides:
+                block = r_all.at[slot, xx, four(z + (4 - n) * step), core]
+                to_partner(0, block, block)
         return 0
 
     def forward_shared(n, _):
@@ -253,25 +267,15 @@
         return 0
 
     lax.fori_loop(0, 4, forward_right, 0)
-    lax.fori_loop(4, 8, forward_shared, 0)
+    def both(n, _):
+        forward_shared(n, 0)
+        return relayed_right(n - 4, 0)
+
+    lax.fori_loop(4, 7, both, 0)
+    forward_shared(7, 0)
     lax.fori_loop(0, 4, left_to, 0)
     lax.fori_loop(4, 6, left_to, 0)
     lax.fori_loop(6, 8, left_near, 0)
-
-    def gates(i, _):
-        gate[i] = jax.nn.sigmoid(jnp.dot(normed[i], w_in[4], preferred_element_type=F32))
-        return 0
-
-    lax.fori_loop(0, ROWS, gates, 0)
-
-    def relayed_right(n, _):
-        block = r_own.at[0, 0, 0]
-        pltpu.make_async_copy(block, block, relay_sem.at[n]).wait()
-        for xx in range(NX):
-            for slot, step in sides:
-                block = r_all.at[slot, xx, four(z + (4 - n) * step), core]
-                to_partner(0, block, block)
-        return 0
 
     def relayed_shared(n, _):
         block = r_own.at[0, 0, 0, pl.ds(0, 16)]
@@ -282,7 +286,7 @@
                 to_partner(1, block, block)
         return 0
 
-    lax.fori_loop(0, 4, relayed_right, 0)
+    relayed_right(3, 0)
     lax.fori_loop(4, 8, relayed_shared, 0)
     sizes = (r_own.at[0, 0], r_own.at[0, 0, pl.ds(0, 2)])
     swaps = (r_own.at[0], r_own.at[0, 0])

time: 54.1 us -> 53.8 us (level)
  no operation moved by 1% of the time
where the time goes in v7:
time: 53.8 us; the launch traced here: 53.7 us
  Pallas kernels  52.9 us (98%)
  local copies, waits for them, and re-layouts  0.82 us (2%)
    pallas_call x1, Pallas kernels, local(): pl.pallas_call(kernel, out_shape=jax.ShapeDtypeStruct((ROWS, COLS, WIDTH)...  52.9 us

profile of v7, /device:TPU:1, one launch (start us, length us, event | category | flops | bytes accessed | tf_op | source)
XLA Modules:
  0.0 53.7 jit_solution(6894262179985990128)
XLA Ops:
  0.0 52.9 %shard_map.82 = bf16[12,192,128]{2,1,0:T(8,128)(2,1)S(1)} custom-call(bf16[12,192,128]{2,1,0:T(8,128)(2,1)} %x_hbm.1, s32[12,12]{1,0:T(8,128)} %tm_hbm.1, bf16[128,128]{1,0:T(8,128)(2,1)} %wlg_hbm.1, bf16[128,128]{1,0:T(8,128)(2,1)} %wl_hbm.1, bf16[128,128]{1,0:T(8,128)(2,1)} %wrg_hbm.1, bf16[128,128]{1,0:T(8,128)(2,1)} %wr_hbm.1, bf16[128,128]{1,0:T(8,128)(2,1)} %wog_hbm.1, ...), custom_call_target="tpu_custom_call" | custom-call | tf_op jit(solution)/shard_map/pallas_call | solution.py:440
  52.9 0.8 %copy.10 = bf16[12,192,128]{2,1,0:T(8,128)(2,1)} copy(bf16[12,192,128]{2,1,0:T(8,128)(2,1)S(1)} %shard_map.82) | data formatting | bytes 1179648

commit v8 on v7

--- a/solution.py
+++ b/solution.py
@@ -381,8 +381,11 @@
         return 0
 
     every = [(dy, dx) for dy in range(NY) for dx in range(NX)]
-    lax.fori_loop(0, 2, lambda slot, _: rows_of(slot, 0, (3,)), 0)
-    lax.fori_loop(0, 2, lambda k, _: send_b(k, every), 0)
+    def farthest(slot, _):
+        rows_of(slot, 0, (3,))
+        return send_b(slot, every)
+
+    lax.fori_loop(0, 2, farthest, 0)
     lax.fori_loop(0, 2, lambda slot, _: rows_of(slot, 1, (2, 1, 0)), 0)
     for slot in range(2):
         pltpu.make_async_copy(t_a.at[slot, q, s], in_a.at[channels[slot]], a_sem).start()

time: 53.8 us -> 53.9 us (level)
  no operation moved by 1% of the time
where the time goes in v8:
time: 53.9 us; the launch traced here: 53.5 us
  Pallas kernels  52.7 us (98%)
  local copies, waits for them, and re-layouts  0.82 us (2%)
    pallas_call x1, Pallas kernels, local(): pl.pallas_call(kernel, out_shape=jax.ShapeDtypeStruct((ROWS, COLS, WIDTH)...  52.7 us

profile of v8, /device:TPU:1, one launch (start us, length us, event | category | flops | bytes accessed | tf_op | source)
XLA Modules:
  0.0 53.5 jit_solution(7603167168606157963)
XLA Ops:
  0.0 52.7 %shard_map.82 = bf16[12,192,128]{2,1,0:T(8,128)(2,1)S(1)} custom-call(bf16[12,192,128]{2,1,0:T(8,128)(2,1)} %x_hbm.1, s32[12,12]{1,0:T(8,128)} %tm_hbm.1, bf16[128,128]{1,0:T(8,128)(2,1)} %wlg_hbm.1, bf16[128,128]{1,0:T(8,128)(2,1)} %wl_hbm.1, bf16[128,128]{1,0:T(8,128)(2,1)} %wrg_hbm.1, bf16[128,128]{1,0:T(8,128)(2,1)} %wr_hbm.1, bf16[128,128]{1,0:T(8,128)(2,1)} %wog_hbm.1, ...), custom_call_target="tpu_custom_call" | custom-call | tf_op jit(solution)/shard_map/pallas_call | solution.py:443
  52.7 0.8 %copy.10 = bf16[12,192,128]{2,1,0:T(8,128)(2,1)} copy(bf16[12,192,128]{2,1,0:T(8,128)(2,1)S(1)} %shard_map.82) | data formatting | bytes 1179648
